TPU v7x, 32 devices: a whole 2x2x4 slice. The times are simulated.
32 devices in a mesh: gx: 4 (over z), gy: 4 (over y, x), gz: 2 (over core).
Axes of the slice: x: 2, y: 2, z: 4, core: 2. Of those that a mesh axis runs over, the one named last changes fastest.
Arguments:
- schur: bfloat16 [4, 4, 2, 2048, 2048], P('gx', 'gy', 'gz'), may hold values from -0.09375 to 0.09375
- interface_diag: float32 [4, 4, 2, 2048], P('gx', 'gy', 'gz'), may hold values from 2 to 4
- precond: float32 [4, 4, 2, 16, 128, 128], P('gx', 'gy', 'gz'), may hold values from -0.3 to 0.8
- load: bfloat16 [4, 4, 2, 2048, 256], P('gx', 'gy', 'gz'), may hold values from -170 to 170
- face_blocks: int32 [4, 4, 2, 6, 2], P('gx', 'gy', 'gz'), may hold values from 0 to 16, as said below
Outputs:
- solution: float32 [4, 4, 2, 2048, 256], P('gx', 'gy', 'gz')
- residual_norm: float32 [256], replicated
Inputs may be any that keep to these rules, and one draw needn't show every extreme that they name: `face_blocks`: for each subdomain p and direction d (0, 1: next and previous along the first grid dimension; 2, 3 and 4, 5 likewise along the second and third), slots 0 to n - 1 hold block numbers below 16 shared with the neighbour in that direction, where n (1 to 2 inside the grid, 0 across its boundary) equals the neighbour's n for the opposite direction, and the neighbour's slot k of the opposite direction holds the block that shares with p's slot k; the remaining slots hold 16; no block number appears twice in one subdomain's table; some face shares 2 blocks in every draw.
All inputs are finite; a program needn't handle non-finite values.
Results may differ from a plain program's by a relative error of at most 0.0008.
Values sent between devices are 32-bit elements; how exact they have to be, the bound alone decides.
A program may use at most 128 MiB of HBM per device.

v0:
```python
import functools

import jax
import jax.numpy as jnp
from jax import lax
from jax.experimental import pallas as pl
from jax.experimental.pallas import tpu as pltpu
from jax.sharding import PartitionSpec as P

EPS = 1e-06
MESH = pl.DeviceIdType.MESH
AXES = ("gx", "gy", "gz")
LANES = 128
F32 = jnp.float32
BF16 = jnp.bfloat16


def kernel(
    sizes,
    load_send,
    prec_send,
    schur_slots,
    diag_slots,
    mask_ref,
    out_ref,
    norm_ref,
    load_recv,
    prec_recv,
    prec_split,
    rhs,
    z1_ref,
    z2_ref,
    z_narrow,
    u1_send,
    u1_recv,
    q_ref,
    u2_send,
    u2_recv,
    plane_buf,
    line_buf,
    face_send,
    face_recv,
    plane_send,
    plane_recv,
    line_send,
    line_recv,
):
    nx, ny, nz = sizes
    planes = ny * nz
    cap, blk = prec_send.shape[1:3]
    cols = load_send.shape[-1]
    slots = 6 * cap
    rows = cap * blk
    gx, gy, gz = (lax.axis_index(a) for a in AXES)
    here = gy * nz + gz

    def plane_peer(step):
        other = lax.rem(here + step, planes)
        return (gx, other // nz, lax.rem(other, nz))

    def line_peer(step):
        return (lax.rem(gx + step, nx), gy, gz)

    barrier = pltpu.get_barrier_semaphore()
    for step in range(1, planes):
        pl.semaphore_signal(barrier, inc=1, device_id=plane_peer(step), device_id_type=MESH)
    for step in range(1, nx):
        pl.semaphore_signal(barrier, inc=1, device_id=line_peer(step), device_id_type=MESH)

    target, has = [], []
    for d in range(6):
        at = [gx, gy, gz]
        if d % 2 == 0:
            has.append(at[d // 2] + 1 < sizes[d // 2])
            at[d // 2] = at[d // 2] + 1
        else:
            has.append(at[d // 2] > 0)
            at[d // 2] = at[d // 2] - 1
        target.append(tuple(at))

    def face_copy(number, source, landing, d, slot):
        return pltpu.make_async_remote_copy(
            src_ref=source,
            dst_ref=landing.at[slot],
            send_sem=face_send.at[number, d],
            recv_sem=face_recv.at[number, slot],
            device_id=target[d],
            device_id_type=MESH,
        )

    def send_face(number, source, landing, d):
        @pl.when(has[d])
        def _():
            face_copy(number, source, landing, d, d ^ 1).start()

    def wait_face(number, source, landing, d):
        @pl.when(has[d])
        def _():
            face_copy(number, source, landing, d, d).wait_recv()

    def wait_sent(number, source, landing, d):
        @pl.when(has[d])
        def _():
            face_copy(number, source, landing, d, d ^ 1).wait_send()

    def reduce_start(number, buf, count, me, peer, send, recv):
        for step in range(1, count):
            pltpu.make_async_remote_copy(
                src_ref=buf.at[number, me],
                dst_ref=buf.at[number, me],
                send_sem=send.at[number, step - 1],
                recv_sem=recv.at[number, step - 1],
                device_id=peer(step),
                device_id_type=MESH,
            ).start()

    def reduce_wait(number, buf, count, me, peer, send, recv, sent):
        for step in range(1, count):
            came = me if sent else lax.rem(me + count - step, count)
            copy = pltpu.make_async_remote_copy(
                src_ref=buf.at[number, me],
                dst_ref=buf.at[number, came],
                send_sem=send.at[number, step - 1],
                recv_sem=recv.at[number, step - 1],
                device_id=peer(step),
                device_id_type=MESH,
            )
            if sent:
                copy.wait_send()
            else:
                copy.wait_recv()

    plane_args = (plane_buf, planes, here, plane_peer, plane_send, plane_recv)
    line_args = (line_buf, nx, gx, line_peer, line_send, line_recv)

    def pack(values):
        parts = []
        for value in values:
            row = jnp.sum(value, axis=0, keepdims=True)
            for j in range(cols // LANES):
                parts.append(row[:, j * LANES : (j + 1) * LANES])
        spare = plane_buf.shape[2] - len(parts)
        if spare:
            parts.append(jnp.zeros((spare, LANES), F32))
        return jnp.concatenate(parts, axis=0)

    def unpack(total, i):
        n = cols // LANES
        return jnp.concatenate([total[i * n + j : i * n + j + 1] for j in range(n)], axis=1)

    def total_of(buf, number, count):
        total = buf[number, 0]
        for i in range(1, count):
            total = total + buf[number, i]
        return total

    def folded(x):
        return jnp.sum(x.reshape(x.shape[0] // 8, 8, cols), axis=0)

    for d in range(6):
        @pl.when(jnp.logical_not(has[d]))
        def _(d=d):
            load_recv[d] = jnp.zeros(load_recv.shape[1:], F32)
            prec_recv[d] = jnp.zeros(prec_recv.shape[1:], F32)
            u1_recv[d] = jnp.zeros(u1_recv.shape[1:], F32)
            u2_recv[d] = jnp.zeros(u2_recv.shape[1:], F32)

    order = (2, 3, 0, 1, 4, 5)
    arrival = (4, 5, 0, 1, 2, 3)
    pl.semaphore_wait(barrier, planes - 1 + nx - 1)
    for d in order:
        send_face(0, load_send.at[d], load_recv, d)
    for d in order:
        send_face(1, prec_send.at[d], prec_recv, d)

    square = jnp.zeros((8, cols), F32)
    for d in arrival:
        wait_face(0, load_send.at[d], load_recv, d)
        value = load_send[d] + load_recv[d]
        rhs[d] = value
        square = square + folded(value * value)

    def precondition(s, value, wide):
        high = value.astype(BF16)
        low = (value - high.astype(F32)).astype(BF16)
        both = prec_split[s]
        z = jnp.dot(both, jnp.concatenate([high, high], axis=0), preferred_element_type=F32)
        z = z + jnp.dot(both[:, :blk], low, preferred_element_type=F32)
        wide[s] = z
        z_narrow[s * blk : (s + 1) * blk] = z.astype(BF16)

    def operate(d, wide):
        product = jnp.dot(
            schur_slots[d * rows : (d + 1) * rows], z_narrow[...], preferred_element_type=F32
        )
        scale = diag_slots[d * rows : (d + 1) * rows]
        scale = jnp.concatenate([scale] * (cols // LANES), axis=1)
        return product + scale * wide[d * cap : (d + 1) * cap].reshape(rows, cols)

    for d in arrival:
        wait_face(1, prec_send.at[d], prec_recv, d)
        for k in range(cap):
            s = d * cap + k
            block = prec_send[d, k] + prec_recv[d, k]
            high = block.astype(BF16)
            low = (block - high.astype(F32)).astype(BF16)
            prec_split[s] = jnp.concatenate([high, low], axis=1)
            precondition(s, rhs[d, k * blk : (k + 1) * blk], z1_ref)
    cross = jnp.zeros((8, cols), F32)
    for d in order:
        value = operate(d, z1_ref)
        u1_send[d] = value
        cross = cross + folded(value * rhs[d])

    plane_buf[0, here] = pack((0.5 * square, cross))
    reduce_start(0, *plane_args)
    for d in (2, 3, 4, 5):
        send_face(2, u1_send.at[d], u1_recv, d)
    reduce_wait(0, *plane_args, False)
    line_buf[0, gx] = total_of(plane_buf, 0, planes)
    reduce_start(0, *line_args)
    for d in (0, 1):
        send_face(2, u1_send.at[d], u1_recv, d)
    reduce_wait(0, *line_args, False)
    total = total_of(line_buf, 0, nx)
    load_square = unpack(total, 0)
    beta_square = load_square + EPS
    beta = jnp.sqrt(beta_square)
    h11 = unpack(total, 1) / beta_square

    square = jnp.zeros((8, cols), F32)
    for d in arrival:
        wait_face(2, u1_send.at[d], u1_recv, d)
        for k in range(cap):
            s = d * cap + k
            part = slice(k * blk, (k + 1) * blk)
            w = (u1_send[d, part] + u1_recv[d, part]) * mask_ref[s, 0:1]
            value = w - h11 * rhs[d, part]
            q_ref[d, part] = value
            square = square + folded(value * value)
            precondition(s, value, z2_ref)
    first = jnp.zeros((8, cols), F32)
    second = jnp.zeros((8, cols), F32)
    half = rows // 2

    def part_sent(d):
        return u2_send.at[d, pl.ds(half if d % 2 == 0 else 0, half)]

    for i, d in enumerate(order):
        value = operate(d, z2_ref)
        u2_send[d] = value
        first = first + folded(value * rhs[d])
        second = second + folded(value * q_ref[d])
        if i:
            send_face(3, part_sent(order[i - 1]), u2_recv, order[i - 1])
    send_face(3, part_sent(order[-1]), u2_recv, order[-1])
    work = jnp.zeros((8, cols), F32)
    step_rows = min(half, blk)
    for d in arrival:
        wait_face(3, part_sent(d), u2_recv, d)
        begin = 0 if d % 2 == 0 else half
        for row in range(0, half, step_rows):
            s = d * cap + (begin + row) // blk
            w = u2_send[d, begin + row : begin + row + step_rows]
            w = (w + u2_recv[d, row : row + step_rows]) * mask_ref[s, 0:1]
            work = work + folded(w * w)

    plane_buf[1, here] = pack((0.5 * square, first, second, work))
    reduce_start(1, *plane_args)
    reduce_wait(1, *plane_args, False)
    line_buf[1, gx] = total_of(plane_buf, 1, planes)
    reduce_start(1, *line_args)
    reduce_wait(1, *line_args, False)
    total = total_of(line_buf, 1, nx)
    q_square = unpack(total, 0)
    inverse = 1.0 / beta
    h21 = jnp.sqrt(q_square * inverse * inverse + EPS)
    t = inverse / h21
    h12 = unpack(total, 1) * t * inverse
    a22 = unpack(total, 2) * t * t
    ww = unpack(total, 3) * t * t
    n1 = load_square * inverse * inverse
    n2 = q_square * t * t
    g12 = h11 * EPS * inverse * t
    h22 = a22 - h12 * g12
    left = (
        ww
        - h12 * h12 * (2.0 - n1)
        - h22 * (2.0 * a22 - h22 * n2)
        + 2.0 * h12 * h22 * g12
    )
    h32 = jnp.sqrt(jnp.maximum(left, 0.0) + EPS)
    r1 = jnp.sqrt(h11 * h11 + h21 * h21)
    c1 = h11 / r1
    s1 = h21 / r1
    top = c1 * h12 + s1 * h22
    low = c1 * h22 - s1 * h12
    r2 = jnp.sqrt(low * low + h32 * h32)
    c2 = low / r2
    s2 = h32 / r2
    y2 = -beta * s1 * c2 / r2
    y1 = (beta * c1 - top * y2) / r1
    norm_ref[...] = beta * s1 * s2
    weight1 = y1 * inverse
    weight2 = y2 * t
    for k in range(slots):
        out_ref[k] = weight1 * z1_ref[k] + weight2 * z2_ref[k]

    for d in range(6):
        wait_sent(0, load_send.at[d], load_recv, d)
        wait_sent(1, prec_send.at[d], prec_recv, d)
        wait_sent(2, u1_send.at[d], u1_recv, d)
        wait_sent(3, part_sent(d), u2_recv, d)
    for number in range(2):
        reduce_wait(number, *plane_args, True)
        reduce_wait(number, *line_args, True)


def gather(table, schur_hbm, diag_ref, precond, load, load_out, prec_out, schur_out, diag_out, mask_out, strips, sems):
    nblk, blk, _ = precond.shape
    cols = load.shape[-1]
    slots = table.shape[0]
    cap = slots // 6
    index = [jnp.minimum(table[s], nblk - 1) for s in range(slots)]
    copies = []
    for s in range(slots):
        at = pl.ds(pl.multiple_of(index[s] * blk, blk), blk)
        copies.append(pltpu.make_async_copy(schur_hbm.at[at], strips.at[s], sems.at[s]))
        copies[-1].start()
    eye = lax.broadcasted_iota(jnp.int32, (blk, blk), 0) == lax.broadcasted_iota(
        jnp.int32, (blk, blk), 1
    )
    for s in range(slots):
        d, k = divmod(s, cap)
        valid = table[s] < nblk
        load_out[d, k * blk : (k + 1) * blk] = jnp.where(valid, load[index[s]].astype(F32), 0.0)
        prec_out[d, k] = precond[index[s]]
        mask_out[s] = jnp.full((8, cols), jnp.where(valid, 1.0, 0.0), F32)
        line = diag_ref[:, pl.ds(pl.multiple_of(index[s] * blk, blk), blk)]
        column = jnp.sum(jnp.where(eye, line, 0.0), axis=1, keepdims=True)
        diag_out[s * blk : (s + 1) * blk] = jnp.broadcast_to(column, (blk, LANES))
    for s in range(slots):
        copies[s].wait()
        for t in range(slots):
            at = pl.ds(pl.multiple_of(index[t] * blk, blk), blk)
            schur_out[s * blk : (s + 1) * blk, t * blk : (t + 1) * blk] = strips[s, :, at]


def place(table, compact, out_ref):
    slots = table.shape[0]
    many = out_ref.shape[0]
    first = pl.program_id(0) * many
    for b in range(many):
        found = jnp.int32(slots)
        for s in range(slots):
            found = jnp.where(table[s] == first + b, jnp.int32(s), found)
        value = compact[jnp.minimum(found, slots - 1)]
        out_ref[b] = jnp.where(found < slots, value, 0.0)


def on_device(sizes, schur, interface_diag, precond, load, face_blocks):
    nblk, blk = precond.shape[3:5]
    cols = load.shape[-1]
    order = schur.shape[-1]
    cap = face_blocks.shape[-1]
    slots = 6 * cap
    rows = cap * blk
    nx, ny, nz = sizes
    planes = ny * nz
    packed = -(-(4 * cols // LANES) // 8) * 8
    vmem = pltpu.VMEM
    dma = pltpu.SemaphoreType.DMA
    anywhere = pl.BlockSpec(memory_space=pl.ANY)
    local = pl.BlockSpec(memory_space=pltpu.VMEM)
    scalars = pl.BlockSpec(memory_space=pltpu.SMEM)
    table = face_blocks.reshape(slots)
    mib = 1024 * 1024
    gathered = pl.pallas_call(
        gather,
        out_shape=(
            jax.ShapeDtypeStruct((6, rows, cols), F32),
            jax.ShapeDtypeStruct((6, cap, blk, blk), F32),
            jax.ShapeDtypeStruct((slots * blk, slots * blk), BF16),
            jax.ShapeDtypeStruct((slots * blk, LANES), F32),
            jax.ShapeDtypeStruct((slots, 8, cols), F32),
        ),
        in_specs=[scalars, anywhere, local, local, local],
        out_specs=(local,) * 5,
        scratch_shapes=[vmem((slots, blk, order), BF16), dma((slots,))],
        compiler_params=pltpu.CompilerParams(vmem_limit_bytes=24 * mib),
    )(
        table,
        schur.reshape(order, order),
        interface_diag.reshape(1, order),
        precond.reshape(nblk, blk, blk),
        load.reshape(nblk, blk, cols),
    )
    compact, norm = pl.pallas_call(
        functools.partial(kernel, sizes),
        out_shape=(
            jax.ShapeDtypeStruct((slots, blk, cols), F32),
            jax.ShapeDtypeStruct((1, cols), F32),
        ),
        in_specs=[local] * 5,
        out_specs=(local, local),
        scratch_shapes=[
            vmem((6, rows, cols), F32),
            vmem((6, cap, blk, blk), F32),
            vmem((slots, blk, 2 * blk), BF16),
            vmem((6, rows, cols), F32),
            vmem((slots, blk, cols), F32),
            vmem((slots, blk, cols), F32),
            vmem((slots * blk, cols), BF16),
            vmem((6, rows, cols), F32),
            vmem((6, rows, cols), F32),
            vmem((6, rows, cols), F32),
            vmem((6, rows, cols), F32),
            vmem((6, rows // 2, cols), F32),
            vmem((2, planes, packed, LANES), F32),
            vmem((2, nx, packed, LANES), F32),
            dma((4, 6)),
            dma((4, 6)),
            dma((2, max(planes - 1, 1))),
            dma((2, max(planes - 1, 1))),
            dma((2, max(nx - 1, 1))),
            dma((2, max(nx - 1, 1))),
        ],
        compiler_params=pltpu.CompilerParams(
            collective_id=0, has_side_effects=True, vmem_limit_bytes=32 * mib
        ),
    )(*gathered)
    many = 4 if nblk % 4 == 0 else 1
    result = pl.pallas_call(
        place,
        grid=(nblk // many,),
        out_shape=jax.ShapeDtypeStruct((nblk, blk, cols), F32),
        in_specs=[scalars, local],
        out_specs=pl.BlockSpec((many, blk, cols), lambda i: (i, 0, 0)),
        compiler_params=pltpu.CompilerParams(vmem_limit_bytes=16 * mib),
    )(table, compact)
    return result.reshape(1, 1, 1, nblk * blk, cols), norm.reshape(cols)


def solution(mesh):
    sizes = tuple(mesh.shape[a] for a in AXES)
    placed = (
        P("gx", "gy", "gz", None, None),
        P("gx", "gy", "gz", None),
        P("gx", "gy", "gz", None, None, None),
        P("gx", "gy", "gz", None, None),
        P("gx", "gy", "gz", None, None),
    )
    return jax.shard_map(
        functools.partial(on_device, sizes),
        mesh=mesh,
        in_specs=placed,
        out_specs=(P("gx", "gy", "gz", None, None), P()),
        check_vma=False,
    )
```

profile of v0, /device:TPU:0, one launch (start us, length us, event | category | flops | bytes accessed | tf_op | source)
XLA Modules:
  0.0 67.1 jit_solution(14255348778140802650)
XLA Ops:
  0.6 0.8 %copy.8 = s32[1,1,1,6,2]{4,3,2,1,0:T(8,128)S(1)} copy(s32[1,1,1,6,2]{3,4,2,1,0:T(2,128)} %param.9) | data formatting | bytes 96 | tf_op args[4]
  1.4 0.1 reshape.25.table
  1.5 0.0 copy-start
  1.5 3.4 %copy-done = bf16[1,1,1,2048,2048]{4,3,2,1,0:T(8,128)(2,1)S(1)} copy-done((bf16[1,1,1,2048,2048]{4,3,2,1,0:T(8,128)(2,1)S(1)}, bf16[1,1,1,2048,2048]{4,3,2,1,0:T(8,128)(2,1)}, u32[]{:S(2)}) %copy-start) | copy-done | bytes 8388632
  4.9 0.0 copy-start.1
  4.9 1.2 %copy-done.1 = f32[1,1,1,16,128,128]{5,4,3,2,1,0:T(8,128)S(1)} copy-done((f32[1,1,1,16,128,128]{5,4,3,2,1,0:T(8,128)S(1)}, f32[1,1,1,16,128,128]{5,4,3,2,1,0:T(8,128)}, u32[]{:S(2)}) %copy-start.1) | copy-done | bytes 1048600
  6.1 0.0 copy-start.2
  6.1 1.2 %copy-done.2 = bf16[1,1,1,2048,256]{4,3,2,1,0:T(8,128)(2,1)S(1)} copy-done((bf16[1,1,1,2048,256]{4,3,2,1,0:T(8,128)(2,1)S(1)}, bf16[1,1,1,2048,256]{4,3,2,1,0:T(8,128)(2,1)}, u32[]{:S(2)}) %copy-start.2) | copy-done | bytes 1048600
  7.3 0.0 copy-start.3
  7.3 0.7 %copy-done.3 = f32[1,1,1,2048]{3,2,1,0:T(1,128)S(1)} copy-done((f32[1,1,1,2048]{3,2,1,0:T(1,128)S(1)}, f32[1,1,1,2048]{3,2,1,0:T(1,128)}, u32[]{:S(2)}) %copy-start.3) | copy-done | bytes 8216
  8.0 2.7 %shard_map.68 = (f32[6,256,256]{2,1,0:T(8,128)S(1)}, f32[6,2,128,128]{3,2,1,0:T(8,128)S(1)}, bf16[1536,1536]{1,0:T(8,128)(2,1)S(1)}, f32[1536,128]{1,0:T(8,128)S(1)}, f32[12,8,256]{2,1,0:T(8,128)S(1)}) custom-call(s32[12]{0:T(128)S(1)} %reshape.25.table, bf16[2048,2048]{1,0:T(8,128)(2,1)S(1)} %bitcast.6, f32[1,2048]{1,0:T(1,128)S(1)} %bitcast.9, ...), custom_call_target="tpu_custom_call" | custom-call | tf_op jit(solution)/shard_map/pallas_call | solution.py:378
  10.7 53.3 %shard_map.69 = (f32[12,128,256]{2,1,0:T(8,128)S(1)}, f32[1,256]{1,0:T(1,128)S(1)}) custom-call(f32[6,256,256]{2,1,0:T(8,128)S(1)} %get-tuple-element.9.load_send, f32[6,2,128,128]{3,2,1,0:T(8,128)S(1)} %get-tuple-element.10.prec_send, bf16[1536,1536]{1,0:T(8,128)(2,1)S(1)} %get-tuple-element.11.schur_slots, f32[1536,128]{1,0:T(8,128)S(1)} %get-tuple-element.12.diag_slots, ...), custom_call_target="tpu_custom_call" | custom-call | tf_op jit(solution)/shard_map/pallas_call | solution.py:398
  64.1 2.5 %shard_map.70 = f32[16,128,256]{2,1,0:T(8,128)} custom-call(s32[12]{0:T(128)S(1)} %reshape.25.table, f32[12,128,256]{2,1,0:T(8,128)S(1)} %get-tuple-element.14.compact), custom_call_target="tpu_custom_call" | custom-call | tf_op jit(solution)/shard_map/pallas_call | solution.py:433
  66.6 0.6 copy.10
Async XLA Ops:
  1.5 3.4 %copy-start = (bf16[1,1,1,2048,2048]{4,3,2,1,0:T(8,128)(2,1)S(1)}, bf16[1,1,1,2048,2048]{4,3,2,1,0:T(8,128)(2,1)}, u32[]{:S(2)}) copy-start(bf16[1,1,1,2048,2048]{4,3,2,1,0:T(8,128)(2,1)} %param.5) | copy-start | bytes 25165828
  4.9 1.2 %copy-start.1 = (f32[1,1,1,16,128,128]{5,4,3,2,1,0:T(8,128)S(1)}, f32[1,1,1,16,128,128]{5,4,3,2,1,0:T(8,128)}, u32[]{:S(2)}) copy-start(f32[1,1,1,16,128,128]{5,4,3,2,1,0:T(8,128)} %param.7) | copy-start | bytes 3145732
  6.1 1.2 %copy-start.2 = (bf16[1,1,1,2048,256]{4,3,2,1,0:T(8,128)(2,1)S(1)}, bf16[1,1,1,2048,256]{4,3,2,1,0:T(8,128)(2,1)}, u32[]{:S(2)}) copy-start(bf16[1,1,1,2048,256]{4,3,2,1,0:T(8,128)(2,1)} %param.8) | copy-start | bytes 3145732
  7.3 0.7 %copy-start.3 = (f32[1,1,1,2048]{3,2,1,0:T(1,128)S(1)}, f32[1,1,1,2048]{3,2,1,0:T(1,128)}, u32[]{:S(2)}) copy-start(f32[1,1,1,2048]{3,2,1,0:T(1,128)} %param.6) | copy-start | bytes 24580
where the time goes:
time: 67.4 us; the launch traced here: 67.1 us
  Pallas kernels  58.5 us (87%)
  local copies, waits for them, and re-layouts  7.94 us (12%)
    pallas_call x1, Pallas kernels, on_device(): pl.pallas_call(functools.partial(kernel, sizes), out_shape=(jax.ShapeDtyp...  53.3 us
    unnamed x10, local copies, waits for them, and re-layouts  7.86 us
    pallas_call x1, Pallas kernels, on_device(): pl.pallas_call(gather, out_shape=(jax.ShapeDtypeStruct((6, rows, cols), F...  2.72 us
    pallas_call x1, Pallas kernels, on_device(): pl.pallas_call(place, grid=(nblk // many,), out_shape=jax.ShapeDtypeStruc...  2.5 us

commit v1 on v0

v1 whole, which is shorter than its diff:
```python
import functools

import jax
import jax.numpy as jnp
from jax import lax
from jax.experimental import pallas as pl
from jax.experimental.pallas import tpu as pltpu
from jax.sharding import PartitionSpec as P

EPS = 1e-06
MESH = pl.DeviceIdType.MESH
AXES = ("gx", "gy", "gz")
LANES = 128
F32 = jnp.float32
BF16 = jnp.bfloat16
ORDER = (2, 3, 0, 1, 4, 5)
NEAR = (4, 5, 0, 1)
FAR = (2, 3)


def kernel(
    sizes,
    table_hbm,
    schur_hbm,
    diag_hbm,
    prec_hbm,
    load_hbm,
    z1_ref,
    z2_ref,
    final_ref,
    table,
    load_all,
    prec_all,
    diag_all,
    schur_all,
    schur_slots,
    diag_slots,
    load_send,
    load_recv,
    prec_send,
    prec_recv,
    prec_split,
    rhs,
    q_ref,
    u1_send,
    u1_recv,
    u2_send,
    u2_recv,
    pass_full,
    pass_half,
    sums,
    plane_one,
    line_one,
    plane_two,
    line_two,
    local_sems,
    face_send,
    face_recv,
    pass_send,
    pass_recv,
    plane_send,
    plane_recv,
    line_send,
    line_recv,
):
    nx, ny, nz = sizes
    planes = ny * nz
    groups, _, rows, lanes = load_send.shape
    nblk, blk = prec_hbm.shape[:2]
    cap = rows // blk
    slots = 6 * cap
    half = rows // 2
    gx, gy, gz = (lax.axis_index(a) for a in AXES)
    here = gy * nz + gz
    relayed = ny == 4 and nz == 2

    moves = [(table_hbm, table), (load_hbm, load_all), (prec_hbm, prec_all), (diag_hbm, diag_all)]
    for b in range(nblk):
        moves.append((schur_hbm.at[:, :, pl.ds(b * blk, blk)], schur_all.at[b]))
    local = [
        pltpu.make_async_copy(source, target, local_sems.at[i])
        for i, (source, target) in enumerate(moves)
    ]
    for copy in local:
        copy.start()

    def plane_peer(step):
        other = lax.rem(here + step, planes)
        return (gx, other // nz, lax.rem(other, nz))

    def line_peer(step):
        return (lax.rem(gx + step, nx), gy, gz)

    barrier = pltpu.get_barrier_semaphore()
    for step in range(1, planes):
        pl.semaphore_signal(barrier, inc=1, device_id=plane_peer(step), device_id_type=MESH)
    for step in range(1, nx):
        pl.semaphore_signal(barrier, inc=1, device_id=line_peer(step), device_id_type=MESH)

    target, has = [], []
    for d in range(6):
        at = [gx, gy, gz]
        if d % 2 == 0:
            has.append(at[d // 2] + 1 < sizes[d // 2])
            at[d // 2] = at[d // 2] + 1
        else:
            has.append(at[d // 2] > 0)
            at[d // 2] = at[d // 2] - 1
        target.append(tuple(at))

    def message(kind, g=0):
        number = {"load": g, "prec": groups, "one": groups + 1 + g, "two": 2 * groups + 1 + g}[kind]
        if kind == "load":
            return number, load_send.at[g], load_recv.at[g], pass_full.at[number], rows, 0
        if kind == "prec":
            return number, prec_send, prec_recv, pass_full.at[number], rows, 0
        if kind == "one":
            return number, u1_send.at[g], u1_recv.at[g], pass_full.at[number], rows, 0
        return number, u2_send.at[g], u2_recv.at[g], pass_half.at[g], half, half

    def parts(d):
        return 2 if relayed and d in FAR else 1

    def sem_of(d, h):
        return 2 * d + h

    def face(msg, d, h, slot, device):
        number, source, landing, _, count, shift = msg
        n = parts(d)
        size = count // n
        begin = (shift if d % 2 == 0 else 0) + h * size
        return pltpu.make_async_remote_copy(
            src_ref=source.at[d, pl.ds(begin, size)],
            dst_ref=landing.at[slot, pl.ds(h * size, size)],
            send_sem=face_send.at[number, sem_of(d, h)],
            recv_sem=face_recv.at[number, sem_of(slot, h)],
            device_id=device,
            device_id_type=MESH,
        )

    def ends(d):
        return (1, 3, 2) if d == 2 else (2, 0, 1)

    def send(msg, d):
        number, source, _, middle, count, shift = msg

        @pl.when(has[d])
        def _():
            if parts(d) == 2:
                first, via, _ = ends(d)
                size = count // 2
                begin = (shift if d % 2 == 0 else 0) + size

                @pl.when(gy == first)
                def _():
                    pltpu.make_async_remote_copy(
                        src_ref=source.at[d, pl.ds(begin, size)],
                        dst_ref=middle,
                        send_sem=face_send.at[number, sem_of(d, 1)],
                        recv_sem=pass_recv.at[number],
                        device_id=(gx, via, gz),
                        device_id_type=MESH,
                    ).start()

                @pl.when(gy != first)
                def _():
                    face(msg, d, 1, d ^ 1, target[d]).start()

            face(msg, d, 0, d ^ 1, target[d]).start()

    def forward(msg, d):
        number, _, landing, middle, count, _ = msg
        size = count // 2
        return pltpu.make_async_remote_copy(
            src_ref=middle,
            dst_ref=landing.at[d ^ 1, pl.ds(size, size)],
            send_sem=pass_send.at[number],
            recv_sem=face_recv.at[number, sem_of(d ^ 1, 1)],
            device_id=(gx, ends(d)[2], gz),
            device_id_type=MESH,
        )

    def relay(msg):
        if not relayed:
            return
        number, _, _, middle, _, _ = msg
        for d in FAR:
            @pl.when(gy == ends(d)[1])
            def _(d=d):
                pltpu.make_async_remote_copy(
                    src_ref=middle,
                    dst_ref=middle,
                    send_sem=pass_send.at[number],
                    recv_sem=pass_recv.at[number],
                    device_id=(gx, ends(d)[0], gz),
                    device_id_type=MESH,
                ).wait_recv()
                forward(msg, d).start()

    def arrived(msg, d):
        for h in range(parts(d)):
            face(msg, d, h, d, target[d]).wait_recv()

    def all_sent(msg):
        for d in range(6):
            @pl.when(has[d])
            def _(d=d):
                for h in range(parts(d)):
                    face(msg, d, h, d ^ 1, target[d]).wait_send()

        if relayed:
            for d in FAR:
                @pl.when(gy == ends(d)[1])
                def _(d=d):
                    forward(msg, d).wait_send()

    def reduce_copy(number, buf, step, slot, me, peer, send_sem, recv_sem):
        return pltpu.make_async_remote_copy(
            src_ref=buf.at[me],
            dst_ref=buf.at[slot],
            send_sem=send_sem.at[number, step - 1],
            recv_sem=recv_sem.at[number, step - 1],
            device_id=peer(step),
            device_id_type=MESH,
        )

    def reduce_start(number, buf, count, me, peer, send_sem, recv_sem):
        for step in range(1, count):
            reduce_copy(number, buf, step, me, me, peer, send_sem, recv_sem).start()

    def reduce_wait(number, buf, count, me, peer, send_sem, recv_sem, sent):
        for step in range(1, count):
            came = me if sent else lax.rem(me + count - step, count)
            copy = reduce_copy(number, buf, step, came, me, peer, send_sem, recv_sem)
            if sent:
                copy.wait_send()
            else:
                copy.wait_recv()

    plane_args = (planes, here, plane_peer, plane_send, plane_recv)
    line_args = (nx, gx, line_peer, line_send, line_recv)

    def plane_of(number):
        return plane_one.at[number] if number < groups else plane_two

    def line_of(number):
        return line_one.at[number] if number < groups else line_two

    def total_of(buf, count):
        total = buf[0]
        for i in range(1, count):
            total = total + buf[i]
        return total

    def reduce_middle(number):
        reduce_wait(number, plane_of(number), *plane_args, False)
        line_of(number)[gx] = total_of(plane_of(number), planes)
        reduce_start(number, line_of(number), *line_args)

    def reduce_end(number):
        reduce_wait(number, line_of(number), *line_args, False)
        return total_of(line_of(number), nx)

    def folded(x):
        return jnp.sum(x.reshape(x.shape[0] // 8, 8, lanes), axis=0)

    def add_sum(g, i, x):
        sums[g, i] = sums[g, i] + x

    local[0].wait()
    picks = [table[s % cap, s // cap] for s in range(slots)]
    index = [jnp.minimum(p, nblk - 1) for p in picks]
    mask = [jnp.minimum(nblk - p, 1).astype(F32) for p in picks]

    def gather_load(g, d):
        for k in range(cap):
            s = d * cap + k
            value = load_all[index[s], :, g * lanes : (g + 1) * lanes].astype(F32)
            load_send[g, d, k * blk : (k + 1) * blk] = value * mask[s]

    def gather_prec(d):
        for k in range(cap):
            prec_send[d, k * blk : (k + 1) * blk] = prec_all[index[d * cap + k]]

    local[1].wait()
    gather_load(0, 2)
    gather_load(0, 3)
    pl.semaphore_wait(barrier, planes - 1 + nx - 1)
    load_0 = message("load", 0)
    prec = message("prec")
    send(load_0, 2)
    gather_load(0, 0)
    send(load_0, 3)
    gather_load(0, 1)
    send(load_0, 0)
    gather_load(0, 4)
    send(load_0, 1)
    gather_load(0, 5)
    send(load_0, 4)
    local[2].wait()
    gather_prec(2)
    send(load_0, 5)
    gather_prec(3)
    send(prec, 2)
    gather_prec(0)
    send(prec, 3)
    gather_prec(1)
    send(prec, 0)
    gather_prec(4)
    send(prec, 1)
    gather_prec(5)
    send(prec, 4)
    for g in range(1, groups):
        for d in range(6):
            gather_load(g, d)
    send(prec, 5)
    sums[...] = jnp.zeros(sums.shape, F32)
    u1_send[...] = jnp.zeros(u1_send.shape, F32)
    u2_send[...] = jnp.zeros(u2_send.shape, F32)
    relay(load_0)
    relay(prec)
    for g in range(1, groups):
        for d in ORDER:
            send(message("load", g), d)

    local[3].wait()
    eye = lax.broadcasted_iota(jnp.int32, (blk, blk), 0) == lax.broadcasted_iota(
        jnp.int32, (blk, blk), 1
    )
    for s in range(slots):
        column = jnp.sum(jnp.where(eye, diag_all[index[s]], 0.0), axis=1, keepdims=True)
        diag_slots[s * blk : (s + 1) * blk] = jnp.broadcast_to(column, (blk, lanes))
    for copy in local[4:]:
        copy.wait()
    for s in range(slots):
        for t in range(slots):
            tile = schur_all[index[t], index[s]]
            schur_slots[s * blk : (s + 1) * blk, t * blk : (t + 1) * blk] = tile
    for g in range(1, groups):
        relay(message("load", g))

    def precondition(s, value):
        high = value.astype(BF16)
        low = (value - high.astype(F32)).astype(BF16)
        top = jnp.concatenate([high, low], axis=1)
        bottom = jnp.concatenate([high, jnp.zeros_like(low)], axis=1)
        z = jnp.dot(
            prec_split[s], jnp.concatenate([top, bottom], axis=0), preferred_element_type=F32
        )
        return z[:, :lanes] + z[:, lanes:]

    def multiply(d, z, into):
        narrow = jnp.concatenate([part.astype(BF16) for part in z], axis=0)
        product = jnp.dot(
            schur_slots[:, d * rows : (d + 1) * rows], narrow, preferred_element_type=F32
        )
        into[...] = into[...] + product.reshape(6, rows, lanes)

    def first_step(g, d):
        @pl.when(has[d])
        def _():
            arrived(message("load", g), d)
            if g == 0:
                arrived(prec, d)
                for k in range(cap):
                    at = slice(k * blk, (k + 1) * blk)
                    block = prec_send[d, at] + prec_recv[d, at]
                    high = block.astype(BF16)
                    low = (block - high.astype(F32)).astype(BF16)
                    prec_split[d * cap + k] = jnp.concatenate([high, low], axis=1)
            z = []
            square = jnp.zeros((8, lanes), F32)
            for k in range(cap):
                at = slice(k * blk, (k + 1) * blk)
                value = load_send[g, d, at] + load_recv[g, d, at]
                rhs[g, d, at] = value
                square = square + folded(value * value)
                z.append(precondition(d * cap + k, value))
                z1_ref[g, d * cap + k] = z[-1]
            add_sum(g, 0, square)
            multiply(d, z, u1_send.at[g])

    def first_done(g):
        for d in ORDER:
            @pl.when(has[d])
            def _(d=d):
                scale = diag_slots[d * rows : (d + 1) * rows]
                z = z1_ref[g, d * cap : (d + 1) * cap].reshape(rows, lanes)
                value = u1_send[g, d] + scale * z
                u1_send[g, d] = value
                add_sum(g, 1, folded(value * rhs[g, d]))

    def pack(values):
        return jnp.concatenate([jnp.sum(v, axis=0, keepdims=True) for v in values], axis=0)

    for g in range(groups):
        for d in NEAR:
            first_step(g, d)
        if g:
            reduce_middle(g - 1)
            relay(message("one", g - 1))
        for d in FAR:
            first_step(g, d)
        first_done(g)
        plane_one[g, here] = pack((0.5 * sums[g, 0], sums[g, 1]))
        reduce_start(g, plane_one.at[g], *plane_args)
        for d in ORDER:
            send(message("one", g), d)

    def second_step(g, d, h11):
        @pl.when(has[d])
        def _():
            arrived(message("one", g), d)
            z = []
            square = jnp.zeros((8, lanes), F32)
            for k in range(cap):
                s = d * cap + k
                at = slice(k * blk, (k + 1) * blk)
                w = (u1_send[g, d, at] + u1_recv[g, d, at]) * mask[s]
                value = w - h11 * rhs[g, d, at]
                q_ref[g, d, at] = value
                square = square + folded(value * value)
                z.append(precondition(s, value))
                z2_ref[g, s] = z[-1]
            add_sum(g, 2, square)
            multiply(d, z, u2_send.at[g])

    def second_done(g):
        for i, d in enumerate(ORDER):
            @pl.when(has[d])
            def _(d=d):
                scale = diag_slots[d * rows : (d + 1) * rows]
                z = z2_ref[g, d * cap : (d + 1) * cap].reshape(rows, lanes)
                value = u2_send[g, d] + scale * z
                u2_send[g, d] = value
                add_sum(g, 3, folded(value * rhs[g, d]))
                add_sum(g, 4, folded(value * q_ref[g, d]))

            if i:
                send(message("two", g), ORDER[i - 1])
        send(message("two", g), ORDER[-1])

    def third_step(g, d):
        @pl.when(has[d])
        def _():
            arrived(message("two", g), d)
            begin = 0 if d % 2 == 0 else half
            work = jnp.zeros((8, lanes), F32)
            size = min(half, blk)
            for row in range(0, half, size):
                w = u2_send[g, d, begin + row : begin + row + size]
                w = (w + u2_recv[g, d, row : row + size]) * mask[d * cap + (begin + row) // blk]
                work = work + folded(w * w)
            add_sum(g, 5, work)

    if groups == 1:
        reduce_middle(0)
        relay(message("one", 0))
    squares, inners = [], []
    for g in range(groups):
        total = reduce_end(g)
        squares.append(total[0:1])
        inners.append(total[1:2] / (total[0:1] + EPS))
        for d in NEAR:
            second_step(g, d, inners[g])
        if g == 0 and groups > 1:
            reduce_middle(groups - 1)
            relay(message("one", groups - 1))
        if g:
            relay(message("two", g - 1))
        for d in FAR:
            second_step(g, d, inners[g])
        second_done(g)

    for g in range(groups):
        for d in NEAR:
            third_step(g, d)
        if g == 0:
            relay(message("two", groups - 1))
        for d in FAR:
            third_step(g, d)

    packed = []
    for g in range(groups):
        packed.append(pack((0.5 * sums[g, 2], sums[g, 3], sums[g, 4], sums[g, 5])))
    plane_two[here] = jnp.concatenate(packed, axis=0)
    reduce_start(groups, plane_two, *plane_args)
    reduce_middle(groups)
    total = reduce_end(groups)
    for g in range(groups):
        q_square, first, second, work = (total[4 * g + i : 4 * g + i + 1] for i in range(4))
        load_square, h11 = squares[g], inners[g]
        beta = jnp.sqrt(load_square + EPS)
        inverse = 1.0 / beta
        h21 = jnp.sqrt(q_square * inverse * inverse + EPS)
        t = inverse / h21
        h12 = first * t * inverse
        a22 = second * t * t
        ww = work * t * t
        n1 = load_square * inverse * inverse
        n2 = q_square * t * t
        g12 = h11 * EPS * inverse * t
        h22 = a22 - h12 * g12
        left = (
            ww
            - h12 * h12 * (2.0 - n1)
            - h22 * (2.0 * a22 - h22 * n2)
            + 2.0 * h12 * h22 * g12
        )
        h32 = jnp.sqrt(jnp.maximum(left, 0.0) + EPS)
        r1 = jnp.sqrt(h11 * h11 + h21 * h21)
        c1 = h11 / r1
        s1 = h21 / r1
        top = c1 * h12 + s1 * h22
        low = c1 * h22 - s1 * h12
        r2 = jnp.sqrt(low * low + h32 * h32)
        c2 = low / r2
        s2 = h32 / r2
        y2 = -beta * s1 * c2 / r2
        y1 = (beta * c1 - top * y2) / r1
        final_ref[3 * g : 3 * g + 1] = y1 * inverse
        final_ref[3 * g + 1 : 3 * g + 2] = y2 * t
        final_ref[3 * g + 2 : 3 * g + 3] = beta * s1 * s2

    for g in range(groups):
        for kind in ("load", "one", "two"):
            all_sent(message(kind, g))
    all_sent(prec)
    for number in range(groups + 1):
        reduce_wait(number, plane_of(number), *plane_args, True)
        reduce_wait(number, line_of(number), *line_args, True)


def place(table_hbm, z1, z2, final, out_ref, norm_ref, buf, norm_buf, table, sems, table_sem):
    groups, slots = z1.shape[:2]
    lanes = z1.shape[-1]
    nblk = out_ref.shape[0]
    cap = slots // 6
    for g in range(groups):
        norm_buf[:, g * lanes : (g + 1) * lanes] = final[3 * g + 2 : 3 * g + 3]
    move = pltpu.make_async_copy(table_hbm, table, table_sem)
    move.start()
    copies = [pltpu.make_async_copy(norm_buf, norm_ref, sems.at[nblk])]
    copies[0].start()
    move.wait()
    picks = [table[s % cap, s // cap] for s in range(slots)]
    for b in range(nblk):
        found = jnp.int32(slots)
        for s in range(slots):
            found = jnp.where(picks[s] == b, jnp.int32(s), found)
        at = jnp.minimum(found, slots - 1)
        for g in range(groups):
            value = final[3 * g : 3 * g + 1] * z1[g, at] + final[3 * g + 1 : 3 * g + 2] * z2[g, at]
            buf[b, :, g * lanes : (g + 1) * lanes] = jnp.where(found < slots, value, 0.0)
        copies.append(pltpu.make_async_copy(buf.at[b], out_ref.at[b], sems.at[b]))
        copies[-1].start()
    for copy in copies:
        copy.wait()


def in_hbm(x):
    return pltpu.with_memory_space_constraint(x, pltpu.HBM)


def on_device(sizes, schur, interface_diag, precond, load, face_blocks):
    nblk, blk = precond.shape[3:5]
    cols = load.shape[-1]
    order = schur.shape[-1]
    cap = face_blocks.shape[-1]
    slots = 6 * cap
    rows = cap * blk
    nx, ny, nz = sizes
    planes = ny * nz
    groups = cols // LANES
    messages = 3 * groups + 1
    vmem = pltpu.VMEM
    dma = pltpu.SemaphoreType.DMA
    hbm = pl.BlockSpec(memory_space=pltpu.HBM)
    local = pl.BlockSpec(memory_space=pltpu.VMEM)
    scalars = pl.BlockSpec(memory_space=pltpu.SMEM)
    table = face_blocks.reshape(6, cap).T
    mib = 1024 * 1024
    z1, z2, final = pl.pallas_call(
        functools.partial(kernel, sizes),
        out_shape=(
            jax.ShapeDtypeStruct((groups, slots, blk, LANES), F32),
            jax.ShapeDtypeStruct((groups, slots, blk, LANES), F32),
            jax.ShapeDtypeStruct((3 * groups, LANES), F32),
        ),
        in_specs=[hbm] * 5,
        out_specs=(local,) * 3,
        scratch_shapes=[
            pltpu.SMEM((cap, 6), jnp.int32),
            vmem((nblk, blk, cols), BF16),
            vmem((nblk, blk, blk), F32),
            vmem((nblk, 1, blk), F32),
            vmem((nblk, nblk, blk, blk), BF16),
            vmem((slots * blk, slots * blk), BF16),
            vmem((slots * blk, LANES), F32),
            vmem((groups, 6, rows, LANES), F32),
            vmem((groups, 6, rows, LANES), F32),
            vmem((6, rows, blk), F32),
            vmem((6, rows, blk), F32),
            vmem((slots, blk, 2 * blk), BF16),
            vmem((groups, 6, rows, LANES), F32),
            vmem((groups, 6, rows, LANES), F32),
            vmem((groups, 6, rows, LANES), F32),
            vmem((groups, 6, rows, LANES), F32),
            vmem((groups, 6, rows, LANES), F32),
            vmem((groups, 6, rows // 2, LANES), F32),
            vmem((2 * groups + 1, rows // 2, LANES), F32),
            vmem((groups, rows // 4, LANES), F32),
            vmem((groups, 6, 8, LANES), F32),
            vmem((groups, planes, 2, LANES), F32),
            vmem((groups, nx, 2, LANES), F32),
            vmem((planes, 4 * groups, LANES), F32),
            vmem((nx, 4 * groups, LANES), F32),
            dma((4 + nblk,)),
            dma((messages, 12)),
            dma((messages, 12)),
            dma((messages,)),
            dma((messages,)),
            dma((groups + 1, max(planes - 1, 1))),
            dma((groups + 1, max(planes - 1, 1))),
            dma((groups + 1, max(nx - 1, 1))),
            dma((groups + 1, max(nx - 1, 1))),
        ],
        compiler_params=pltpu.CompilerParams(
            collective_id=0, has_side_effects=True, vmem_limit_bytes=48 * mib
        ),
    )(
        in_hbm(table),
        in_hbm(schur.reshape(nblk, blk, order)),
        in_hbm(interface_diag.reshape(nblk, 1, blk)),
        in_hbm(precond.reshape(nblk, blk, blk)),
        in_hbm(load.reshape(nblk, blk, cols)),
    )
    result, norm = pl.pallas_call(
        place,
        out_shape=(
            jax.ShapeDtypeStruct((nblk, blk, cols), F32),
            jax.ShapeDtypeStruct((1, cols), F32),
        ),
        in_specs=[hbm, local, local, local],
        out_specs=(hbm, hbm),
        scratch_shapes=[vmem((nblk, blk, cols), F32), vmem((1, cols), F32), pltpu.SMEM((cap, 6), jnp.int32), dma((nblk + 1,)), dma(())],
        compiler_params=pltpu.CompilerParams(vmem_limit_bytes=16 * mib),
    )(in_hbm(table), z1, z2, final)
    return result.reshape(1, 1, 1, nblk * blk, cols), norm.reshape(cols)


def solution(mesh):
    sizes = tuple(mesh.shape[a] for a in AXES)
    placed = (
        P("gx", "gy", "gz", None, None),
        P("gx", "gy", "gz", None),
        P("gx", "gy", "gz", None, None, None),
        P("gx", "gy", "gz", None, None),
        P("gx", "gy", "gz", None, None),
    )
    return jax.shard_map(
        functools.partial(on_device, sizes),
        mesh=mesh,
        in_specs=placed,
        out_specs=(P("gx", "gy", "gz", None, None), P()),
        check_vma=False,
    )
```

time: 67.4 us -> 49.3 us (0.73)
  Pallas kernels: 58.5 us -> 48.5 us
  local copies, waits for them, and re-layouts: 7.94 us -> 0 us
    unnamed x10 -> x0, local copies, waits for them, and re-layouts: 7.86 us -> none
    pallas_call x1, Pallas kernels: 53.3 us -> 46.3 us  [on_device(): pl.pallas_call(functools.partial(kernel, sizes), out_shape=(jax.ShapeDtyp...]
    pallas_call x2 -> x1, Pallas kernels: 5.22 us -> 2.18 us  [on_device(): pl.pallas_call(place, out_shape=(jax.ShapeDtypeStruct((nblk, blk, cols),...]
where the time goes in v1:
time: 49.3 us; the launch traced here: 49.1 us
  Pallas kernels  48.5 us (98%)
  between operations  0.64 us (1%)
    pallas_call x1, Pallas kernels, on_device(): pl.pallas_call(functools.partial(kernel, sizes), out_shape=(jax.ShapeDtyp...  46.3 us
    pallas_call x1, Pallas kernels, on_device(): pl.pallas_call(place, out_shape=(jax.ShapeDtypeStruct((nblk, blk, cols),...  2.18 us

profile of v1, /device:TPU:0, one launch (start us, length us, event | category | flops | bytes accessed | tf_op | source)
XLA Modules:
  0.0 49.1 jit_solution(13184777663030792640)
XLA Ops:
  0.6 46.3 %shard_map.68 = (f32[2,12,128,128]{3,2,1,0:T(8,128)S(1)}, f32[2,12,128,128]{3,2,1,0:T(8,128)S(1)}, f32[6,128]{1,0:T(8,128)S(1)}) custom-call(s32[2,6]{1,0:T(2,128)} %bitcast.13, bf16[16,128,2048]{2,1,0:T(8,128)(2,1)} %bitcast.9, f32[16,1,128]{2,1,0:T(1,128)} %bitcast.12, f32[16,128,128]{2,1,0:T(8,128)} %bitcast.10, bf16[16,128,256]{2,1,0:T(8,128)(2,1)} %bitcast.11), custom_call_target="tpu_custom_call" | custom-call | tf_op jit(solution)/shard_map/pallas_call | solution.py:583
  46.9 2.2 %shard_map.69 = (f32[16,128,256]{2,1,0:T(8,128)}, f32[1,256]{1,0:T(1,128)}) custom-call(s32[2,6]{1,0:T(2,128)} %bitcast.14, f32[2,12,128,128]{3,2,1,0:T(8,128)S(1)} %get-tuple-element.7.z1, f32[2,12,128,128]{3,2,1,0:T(8,128)S(1)} %get-tuple-element.8.z2, f32[6,128]{1,0:T(8,128)S(1)} %get-tuple-element.9.final), custom_call_target="tpu_custom_call" | custom-call | tf_op jit(solution)/shard_map/pallas_call | solution.py:638

commit v2 on v1

v2 whole, which is shorter than its diff:
```python
import functools

import jax
import jax.numpy as jnp
from jax import lax
from jax.experimental import pallas as pl
from jax.experimental.pallas import tpu as pltpu
from jax.sharding import PartitionSpec as P

EPS = 1e-06
MESH = pl.DeviceIdType.MESH
AXES = ("gx", "gy", "gz")
LANES = 128
F32 = jnp.float32
BF16 = jnp.bfloat16
ORDER = (2, 3, 0, 1, 4, 5)
NEAR = (4, 5, 0, 1)
FAR = (2, 3)
ALL = (0, 1, 2, 3, 4, 5)


def kernel(
    sizes,
    table_hbm,
    schur_hbm,
    diag_hbm,
    prec_hbm,
    load_hbm,
    z1_out,
    z2_out,
    final_ref,
    table,
    load_all,
    prec_all,
    diag_all,
    schur_all,
    schur_slots,
    diag_slots,
    first_send,
    first_recv,
    load_send,
    load_recv,
    prec_split,
    rhs,
    a_ref,
    z1_ref,
    z2_ref,
    u1_send,
    u1_recv,
    u2_send,
    u2_recv,
    pass_first,
    pass_full,
    pass_half,
    pass_last,
    sums,
    plane_one,
    line_one,
    plane_two,
    line_two,
    local_sems,
    face_send,
    face_recv,
    pass_send,
    pass_recv,
    plane_send,
    plane_recv,
    line_send,
    line_recv,
):
    nx, ny, nz = sizes
    planes = ny * nz
    groups, _, rows, lanes = rhs.shape
    nblk, blk = prec_hbm.shape[:2]
    cap = rows // blk
    slots = 6 * cap
    half = rows // 2
    gx, gy, gz = (lax.axis_index(a) for a in AXES)
    here = gy * nz + gz
    relayed = ny == 4 and nz == 2

    moves = [(table_hbm, table), (load_hbm, load_all), (prec_hbm, prec_all), (diag_hbm, diag_all)]
    local = [
        pltpu.make_async_copy(source, target, local_sems.at[i])
        for i, (source, target) in enumerate(moves)
    ]
    for copy in local:
        copy.start()
    for b in range(nblk):
        pltpu.make_async_copy(
            schur_hbm.at[:, :, pl.ds(b * blk, blk)], schur_all.at[b], local_sems.at[4]
        ).start()

    def plane_peer(step):
        other = lax.rem(here + step, planes)
        return (gx, other // nz, lax.rem(other, nz))

    def line_peer(step):
        return (lax.rem(gx + step, nx), gy, gz)

    target, has = [], []
    for d in range(6):
        at = [gx, gy, gz]
        if d % 2 == 0:
            has.append(at[d // 2] + 1 < sizes[d // 2])
            at[d // 2] = at[d // 2] + 1
        else:
            has.append(at[d // 2] > 0)
            at[d // 2] = at[d // 2] - 1
        target.append(tuple(at))

    barrier = pltpu.get_barrier_semaphore()
    near = relayed and nx <= 4
    entered = jnp.int32(1)
    if near:
        for d in range(6):
            entered = entered + has[d].astype(jnp.int32)

            @pl.when(has[d])
            def _(d=d):
                pl.semaphore_signal(barrier, inc=1, device_id=target[d], device_id_type=MESH)

        pl.semaphore_signal(
            barrier, inc=1, device_id=(gx, lax.rem(gy + 2, ny), gz), device_id_type=MESH
        )
    else:
        entered = planes - 1 + nx - 1
        for step in range(1, planes):
            pl.semaphore_signal(barrier, inc=1, device_id=plane_peer(step), device_id_type=MESH)
        for step in range(1, nx):
            pl.semaphore_signal(barrier, inc=1, device_id=line_peer(step), device_id_type=MESH)

    def message(kind, g):
        if kind == "load" and g == 0:
            return g, g, first_send, first_recv, pass_first, 2 * rows, 0, rows
        if kind == "load":
            return g, g, load_send.at[g - 1], load_recv.at[g - 1], pass_full.at[g - 1], rows, 0, half
        if kind == "one":
            middle = pass_full.at[groups - 1 + g]
            return g, groups + g, u1_send.at[g], u1_recv.at[g], middle, rows, 0, half
        if g == groups - 1:
            return g, g, u2_send.at[g], u2_recv.at[g], pass_last, half, half, half // 4
        return g, g, u2_send.at[g], u2_recv.at[g], pass_half.at[g], half, half, half // 2

    def before(kind, g):
        return {"load": None, "one": ("load", g), "two": ("one", g)}[kind]

    def ends(d):
        return (1, 3, 2) if d == 2 else (2, 0, 1)

    def face(msg, d, slot, device, row=0, size=None):
        g, number, source, landing, _, count, shift, _ = msg
        size = size or count
        begin = (shift if d % 2 == 0 else 0) + row
        return pltpu.make_async_remote_copy(
            src_ref=source.at[d, pl.ds(begin, size)],
            dst_ref=landing.at[slot, pl.ds(row, size)],
            send_sem=face_send.at[g, d],
            recv_sem=face_recv.at[number, slot],
            device_id=device,
            device_id_type=MESH,
        )

    def to_relay(msg, d):
        g, number, source, _, middle, count, shift, via = msg
        begin = (shift if d % 2 == 0 else 0) + count - via
        return pltpu.make_async_remote_copy(
            src_ref=source.at[d, pl.ds(begin, via)],
            dst_ref=middle,
            send_sem=face_send.at[g, d],
            recv_sem=pass_recv.at[number],
            device_id=(gx, ends(d)[1], gz),
            device_id_type=MESH,
        )

    def sent(msg, d):
        face(msg, d, d ^ 1, target[d]).wait_send()

    def send(kind, g, d):
        msg = message(kind, g)
        count, via = msg[5], msg[7]

        @pl.when(has[d])
        def _():
            if before(kind, g):
                sent(message(*before(kind, g)), d)
            if relayed and d in FAR:
                @pl.when(gy == ends(d)[0])
                def _():
                    to_relay(msg, d).start()
                    face(msg, d, d ^ 1, target[d], 0, count - via).start()

                @pl.when(gy != ends(d)[0])
                def _():
                    face(msg, d, d ^ 1, target[d]).start()
            else:
                face(msg, d, d ^ 1, target[d]).start()

    def forward(msg, d):
        g, number, _, landing, middle, count, _, via = msg
        return pltpu.make_async_remote_copy(
            src_ref=middle,
            dst_ref=landing.at[d ^ 1, pl.ds(count - via, via)],
            send_sem=pass_send.at[g],
            recv_sem=face_recv.at[number, d ^ 1],
            device_id=(gx, ends(d)[2], gz),
            device_id_type=MESH,
        )

    def relay(kind, g):
        if not relayed:
            return
        msg = message(kind, g)
        for d in FAR:
            @pl.when(gy == ends(d)[1])
            def _(d=d):
                to_relay(msg, d).wait_recv()
                if before(kind, g):
                    forward(message(*before(kind, g)), d).wait_send()
                forward(msg, d).start()

    def arrived(kind, g, d):
        face(message(kind, g), d, d, target[d]).wait_recv()

    def all_sent(kind, g):
        msg = message(kind, g)
        for d in range(6):
            @pl.when(has[d])
            def _(d=d):
                sent(msg, d)

        if relayed:
            for d in FAR:
                @pl.when(gy == ends(d)[1])
                def _(d=d):
                    forward(msg, d).wait_send()

    def reduce_start(number, buf, count, me, peer, send_sem, recv_sem):
        for step in range(1, count):
            pltpu.make_async_remote_copy(
                src_ref=buf.at[me],
                dst_ref=buf.at[me],
                send_sem=send_sem.at[number],
                recv_sem=recv_sem.at[number],
                device_id=peer(step),
                device_id_type=MESH,
            ).start()

    def reduce_wait(number, buf, count, me, peer, send_sem, recv_sem, sent):
        if count > 1:
            copy = pltpu.make_async_remote_copy(
                src_ref=buf.at[pl.ds(0, count - 1)],
                dst_ref=buf.at[pl.ds(0, count - 1)],
                send_sem=send_sem.at[number],
                recv_sem=recv_sem.at[number],
                device_id=peer(1),
                device_id_type=MESH,
            )
            if sent:
                copy.wait_send()
            else:
                copy.wait_recv()

    plane_args = (planes, here, plane_peer, plane_send, plane_recv)
    line_args = (nx, gx, line_peer, line_send, line_recv)

    def plane_of(number):
        return plane_two if number else plane_one

    def line_of(number):
        return line_two if number else line_one

    def total_of(buf, count):
        total = buf[0]
        for i in range(1, count):
            total = total + buf[i]
        return total

    def reduce_middle(number):
        reduce_wait(number, plane_of(number), *plane_args, False)
        line_of(number)[gx] = total_of(plane_of(number), planes)
        reduce_start(number, line_of(number), *line_args)

    def reduce_end(number):
        reduce_wait(number, line_of(number), *line_args, False)
        return total_of(line_of(number), nx)

    def folded(x):
        return jnp.sum(x.reshape(x.shape[0] // 8, 8, lanes), axis=0)

    def add_sum(g, i, x):
        sums[g, i] = sums[g, i] + x

    local[0].wait()
    picks = [table[s % cap, s // cap] for s in range(slots)]
    index = [jnp.minimum(p, nblk - 1) for p in picks]
    mask = [jnp.minimum(nblk - p, 1).astype(F32) for p in picks]

    def gather_load(g, d):
        for k in range(cap):
            s = d * cap + k
            value = load_all[index[s], :, g * lanes : (g + 1) * lanes].astype(F32)
            if g:
                load_send[g - 1, d, k * blk : (k + 1) * blk] = value * mask[s]
            else:
                first_send[d, k * blk : (k + 1) * blk] = value * mask[s]

    def gather_prec(d):
        for k in range(cap):
            at = slice(rows + k * blk, rows + (k + 1) * blk)
            first_send[d, at] = prec_all[index[d * cap + k]]

    local[1].wait()
    for d in FAR:
        gather_load(0, d)
    local[2].wait()
    for d in FAR:
        gather_prec(d)
    gather_load(0, 0)
    gather_prec(0)
    pl.semaphore_wait(barrier, entered)
    for d in FAR:
        send("load", 0, d)
    gather_load(0, 1)
    gather_prec(1)
    send("load", 0, 0)
    gather_load(0, 4)
    gather_prec(4)
    send("load", 0, 1)
    gather_load(0, 5)
    gather_prec(5)
    send("load", 0, 4)
    for g in range(1, groups):
        for d in range(6):
            gather_load(g, d)
    send("load", 0, 5)
    sums[...] = jnp.zeros(sums.shape, F32)
    for d in range(6):
        @pl.when(jnp.logical_not(has[d]))
        def _(d=d):
            for g in range(groups):
                blank = jnp.zeros((cap, blk, lanes), F32)
                z1_ref[g, d * cap : (d + 1) * cap] = blank
                z2_ref[g, d * cap : (d + 1) * cap] = blank

    u1_send[...] = jnp.zeros(u1_send.shape, F32)
    u2_send[...] = jnp.zeros(u2_send.shape, F32)
    local[3].wait()
    eye = lax.broadcasted_iota(jnp.int32, (blk, blk), 0) == lax.broadcasted_iota(
        jnp.int32, (blk, blk), 1
    )
    for s in range(slots):
        column = jnp.sum(jnp.where(eye, diag_all[index[s]], 0.0), axis=1, keepdims=True)
        diag_slots[s * blk : (s + 1) * blk] = jnp.broadcast_to(column, (blk, lanes))
    relay("load", 0)
    for g in range(1, groups):
        for d in ORDER:
            send("load", g, d)
    pltpu.make_async_copy(schur_all, schur_all, local_sems.at[4]).wait()
    for s in range(slots):
        for t in range(slots):
            tile = schur_all[index[t], index[s]]
            schur_slots[s * blk : (s + 1) * blk, t * blk : (t + 1) * blk] = tile
    for g in range(1, groups):
        relay("load", g)

    def precondition(s, value):
        high = value.astype(BF16)
        low = (value - high.astype(F32)).astype(BF16)
        top = jnp.concatenate([high, low], axis=1)
        bottom = jnp.concatenate([high, jnp.zeros_like(low)], axis=1)
        z = jnp.dot(
            prec_split[s], jnp.concatenate([top, bottom], axis=0), preferred_element_type=F32
        )
        return z[:, :lanes] + z[:, lanes:]

    def narrowed(z):
        return jnp.concatenate([part.astype(BF16) for part in z], axis=0)

    def multiply(d, narrow, into, which):
        first, last = which[0], which[-1] + 1
        product = jnp.dot(
            schur_slots[first * rows : last * rows, d * rows : (d + 1) * rows],
            narrow,
            preferred_element_type=F32,
        )
        into[first:last] = into[first:last] + product.reshape(last - first, rows, lanes)

    def columns_of(z_ref, g, d):
        return narrowed([z_ref[g, d * cap + k] for k in range(cap)])

    def first_step(g, d):
        @pl.when(has[d])
        def _():
            arrived("load", g, d)
            if g == 0:
                for k in range(cap):
                    at = slice(rows + k * blk, rows + (k + 1) * blk)
                    block = first_send[d, at] + first_recv[d, at]
                    high = block.astype(BF16)
                    low = (block - high.astype(F32)).astype(BF16)
                    prec_split[d * cap + k] = jnp.concatenate([high, low], axis=1)
            z = []
            square = jnp.zeros((8, lanes), F32)
            for k in range(cap):
                at = slice(k * blk, (k + 1) * blk)
                if g:
                    value = load_send[g - 1, d, at] + load_recv[g - 1, d, at]
                else:
                    value = first_send[d, at] + first_recv[d, at]
                rhs[g, d, at] = value
                square = square + folded(value * value)
                z.append(precondition(d * cap + k, value))
                z1_ref[g, d * cap + k] = z[-1]
            add_sum(g, 0, square)
            multiply(d, narrowed(z), u1_send.at[g], ALL if d in NEAR else FAR)

    def second_step(g, d):
        @pl.when(has[d])
        def _():
            arrived("one", g, d)
            z = []
            for k in range(cap):
                s = d * cap + k
                at = slice(k * blk, (k + 1) * blk)
                value = (u1_send[g, d, at] + u1_recv[g, d, at]) * mask[s]
                a_ref[g, d, at] = value
                z.append(precondition(s, value))
                z2_ref[g, s] = z[-1]
            multiply(d, narrowed(z), u2_send.at[g], ALL if d in NEAR else FAR)

    def add_diagonal(z_ref, u_ref, g, d):
        scale = diag_slots[d * rows : (d + 1) * rows]
        u_ref[g, d] = u_ref[g, d] + scale * z_ref[g, d * cap : (d + 1) * cap].reshape(rows, lanes)

    def finish_far(g, z_ref, u_ref, kind):
        for d in FAR:
            @pl.when(has[d])
            def _(d=d):
                add_diagonal(z_ref, u_ref, g, d)

        for d in FAR:
            send(kind, g, d)

    def finish_near(g, z_ref, u_ref, kind):
        for d in FAR:
            @pl.when(has[d])
            def _(d=d):
                narrow = columns_of(z_ref, g, d)
                multiply(d, narrow, u_ref.at[g], (0, 1))
                multiply(d, narrow, u_ref.at[g], (4, 5))

        for d in (0, 1, 4, 5):
            @pl.when(has[d])
            def _(d=d):
                add_diagonal(z_ref, u_ref, g, d)

        for d in (0, 1, 4, 5):
            send(kind, g, d)

    def cross(g):
        for d in range(6):
            @pl.when(has[d])
            def _(d=d):
                add_sum(g, 1, folded(u1_send[g, d] * rhs[g, d]))

    def pack(values):
        return jnp.concatenate([jnp.sum(v, axis=0, keepdims=True) for v in values], axis=0)

    place = []
    for b in range(nblk):
        slot, live = jnp.int32(0), jnp.int32(0)
        for s in range(slots):
            same = 1 - jnp.minimum(jnp.abs(picks[s] - b), 1)
            slot, live = slot + s * same, live + same
        place.append((jnp.minimum(slot, slots - 1), live.astype(F32)))

    def spread(g, z_ref, z_out):
        for b in range(nblk):
            slot, live = place[b]
            z_out[b, :, g * lanes : (g + 1) * lanes] = z_ref[g, slot] * live

    last = groups - 1
    for g in range(groups):
        for d in NEAR:
            first_step(g, d)
        if g:
            relay("one", g - 1)
        for d in FAR:
            first_step(g, d)
        finish_far(g, z1_ref, u1_send, "one")
        finish_near(g, z1_ref, u1_send, "one")
        cross(g)
        spread(g, z1_ref, z1_out)

    for g in range(groups):
        if groups == 1:
            relay("one", last)
        for d in NEAR:
            second_step(g, d)
        if g == 0:
            packed = [pack((0.5 * sums[i, 0], sums[i, 1])) for i in range(groups)]
            plane_one[here] = jnp.concatenate(packed, axis=0)
            reduce_start(0, plane_one, *plane_args)
            if groups > 1:
                relay("one", last)
        else:
            relay("two", g - 1)
        for d in FAR:
            second_step(g, d)
        finish_far(g, z2_ref, u2_send, "two")
        if g == last:
            reduce_middle(0)
        finish_near(g, z2_ref, u2_send, "two")

    def measure(g, h11):
        for d in range(6):
            @pl.when(has[d])
            def _(d=d):
                square = jnp.zeros((8, lanes), F32)
                first = jnp.zeros((8, lanes), F32)
                second = jnp.zeros((8, lanes), F32)
                for k in range(cap):
                    at = slice(k * blk, (k + 1) * blk)
                    v = rhs[g, d, at]
                    q = a_ref[g, d, at] - h11 * v
                    u = u2_send[g, d, at] - h11 * u1_send[g, d, at]
                    square = square + folded(q * q)
                    first = first + folded(u * v)
                    second = second + folded(u * q)
                add_sum(g, 2, square)
                add_sum(g, 3, first)
                add_sum(g, 4, second)

    def third_step(g, d, h11):
        @pl.when(has[d])
        def _():
            arrived("two", g, d)
            begin = 0 if d % 2 == 0 else half
            work = jnp.zeros((8, lanes), F32)
            size = min(half, blk)
            for row in range(0, half, size):
                at = slice(begin + row, begin + row + size)
                w = (u2_send[g, d, at] + u2_recv[g, d, row : row + size]) * mask[d * cap + (begin + row) // blk]
                w = w - h11 * a_ref[g, d, at]
                work = work + folded(w * w)
            add_sum(g, 5, work)

    spread(0, z2_ref, z2_out)
    relay("two", last)
    total = reduce_end(0)
    squares = [total[2 * g : 2 * g + 1] for g in range(groups)]
    inners = [total[2 * g + 1 : 2 * g + 2] / (squares[g] + EPS) for g in range(groups)]
    measure(0, inners[0])
    for g in range(1, groups):
        spread(g, z2_ref, z2_out)
        measure(g, inners[g])
    for g in range(groups):
        for d in NEAR:
            third_step(g, d, inners[g])
        for d in FAR:
            third_step(g, d, inners[g])

    packed = []
    for g in range(groups):
        packed.append(pack((0.5 * sums[g, 2], sums[g, 3], sums[g, 4], sums[g, 5])))
    plane_two[here] = jnp.concatenate(packed, axis=0)
    reduce_start(1, plane_two, *plane_args)
    for g in range(groups):
        all_sent("two", g)
    reduce_wait(0, plane_one, *plane_args, True)
    reduce_wait(0, line_one, *line_args, True)
    reduce_middle(1)
    reduce_wait(1, plane_two, *plane_args, True)
    total = reduce_end(1)

    def both(rows_of):
        return jnp.concatenate(rows_of, axis=1)

    q_square, first, second, work = (
        both([total[4 * g + i : 4 * g + i + 1] for g in range(groups)]) for i in range(4)
    )
    load_square, h11 = both(squares), both(inners)
    beta = jnp.sqrt(load_square + EPS)
    inverse = 1.0 / beta
    h21 = jnp.sqrt(q_square * inverse * inverse + EPS)
    t = inverse / h21
    h12 = first * t * inverse
    a22 = second * t * t
    ww = work * t * t
    n1 = load_square * inverse * inverse
    n2 = q_square * t * t
    g12 = h11 * EPS * inverse * t
    h22 = a22 - h12 * g12
    left = (
        ww
        - h12 * h12 * (2.0 - n1)
        - h22 * (2.0 * a22 - h22 * n2)
        + 2.0 * h12 * h22 * g12
    )
    h32 = jnp.sqrt(jnp.maximum(left, 0.0) + EPS)
    r1 = jnp.sqrt(h11 * h11 + h21 * h21)
    c1 = h11 / r1
    s1 = h21 / r1
    top = c1 * h12 + s1 * h22
    low = c1 * h22 - s1 * h12
    r2 = jnp.sqrt(low * low + h32 * h32)
    c2 = low / r2
    s2 = h32 / r2
    y2 = -beta * s1 * c2 / r2
    y1 = (beta * c1 - top * y2) / r1
    weight2 = y2 * t
    final_ref[0:1] = y1 * inverse - weight2 * h11
    final_ref[1:2] = weight2
    final_ref[2:3] = beta * s1 * s2
    reduce_wait(1, line_two, *line_args, True)


def combine(z1, z2, final, out_ref, norm_ref, buf, norm_buf, sems):
    nblk = out_ref.shape[0]
    norm_buf[...] = final[2:3]
    copies = [pltpu.make_async_copy(norm_buf, norm_ref, sems.at[nblk])]
    copies[0].start()
    for b in range(nblk):
        buf[b] = final[0:1] * z1[b] + final[1:2] * z2[b]
        copies.append(pltpu.make_async_copy(buf.at[b], out_ref.at[b], sems.at[b]))
        copies[-1].start()
    for copy in copies:
        copy.wait()


def in_hbm(x):
    return pltpu.with_memory_space_constraint(x, pltpu.HBM)


def on_device(sizes, schur, interface_diag, precond, load, face_blocks):
    nblk, blk = precond.shape[3:5]
    cols = load.shape[-1]
    order = schur.shape[-1]
    cap = face_blocks.shape[-1]
    slots = 6 * cap
    rows = cap * blk
    nx, ny, nz = sizes
    planes = ny * nz
    groups = cols // LANES
    vmem = pltpu.VMEM
    dma = pltpu.SemaphoreType.DMA
    hbm = pl.BlockSpec(memory_space=pltpu.HBM)
    local = pl.BlockSpec(memory_space=pltpu.VMEM)
    scalars = pl.BlockSpec(memory_space=pltpu.SMEM)
    table = face_blocks.reshape(6, cap).T
    mib = 1024 * 1024
    z1, z2, final = pl.pallas_call(
        functools.partial(kernel, sizes),
        out_shape=(
            jax.ShapeDtypeStruct((nblk, blk, cols), F32),
            jax.ShapeDtypeStruct((nblk, blk, cols), F32),
            jax.ShapeDtypeStruct((3, cols), F32),
        ),
        in_specs=[hbm] * 5,
        out_specs=(local,) * 3,
        scratch_shapes=[
            pltpu.SMEM((cap, 6), jnp.int32),
            vmem((nblk, blk, cols), BF16),
            vmem((nblk, blk, blk), F32),
            vmem((nblk, 1, blk), F32),
            vmem((nblk, nblk, blk, blk), BF16),
            vmem((slots * blk, slots * blk), BF16),
            vmem((slots * blk, LANES), F32),
            vmem((6, 2 * rows, LANES), F32),
            vmem((6, 2 * rows, LANES), F32),
            vmem((max(groups - 1, 1), 6, rows, LANES), F32),
            vmem((max(groups - 1, 1), 6, rows, LANES), F32),
            vmem((slots, blk, 2 * blk), BF16),
            vmem((groups, 6, rows, LANES), F32),
            vmem((groups, 6, rows, LANES), F32),
            vmem((groups, slots, blk, LANES), F32),
            vmem((groups, slots, blk, LANES), F32),
            vmem((groups, 6, rows, LANES), F32),
            vmem((groups, 6, rows, LANES), F32),
            vmem((groups, 6, rows, LANES), F32),
            vmem((groups, 6, rows // 2, LANES), F32),
            vmem((rows, LANES), F32),
            vmem((2 * groups - 1, rows // 2, LANES), F32),
            vmem((max(groups - 1, 1), rows // 4, LANES), F32),
            vmem((rows // 8, LANES), F32),
            vmem((groups, 6, 8, LANES), F32),
            vmem((planes, 2 * groups, LANES), F32),
            vmem((nx, 2 * groups, LANES), F32),
            vmem((planes, 4 * groups, LANES), F32),
            vmem((nx, 4 * groups, LANES), F32),
            dma((5,)),
            dma((groups, 6)),
            dma((2 * groups, 6)),
            dma((groups,)),
            dma((2 * groups,)),
            dma((2,)),
            dma((2,)),
            dma((2,)),
            dma((2,)),
        ],
        compiler_params=pltpu.CompilerParams(
            collective_id=0, has_side_effects=True, vmem_limit_bytes=44 * mib
        ),
    )(
        in_hbm(table),
        in_hbm(schur.reshape(nblk, blk, order)),
        in_hbm(interface_diag.reshape(nblk, 1, blk)),
        in_hbm(precond.reshape(nblk, blk, blk)),
        in_hbm(load.reshape(nblk, blk, cols)),
    )
    result, norm = pl.pallas_call(
        combine,
        out_shape=(
            jax.ShapeDtypeStruct((nblk, blk, cols), F32),
            jax.ShapeDtypeStruct((1, cols), F32),
        ),
        in_specs=[local, local, local],
        out_specs=(hbm, hbm),
        scratch_shapes=[vmem((nblk, blk, cols), F32), vmem((1, cols), F32), dma((nblk + 1,))],
        compiler_params=pltpu.CompilerParams(vmem_limit_bytes=16 * mib),
    )(z1, z2, final)
    return result.reshape(1, 1, 1, nblk * blk, cols), norm.reshape(cols)


def solution(mesh):
    sizes = tuple(mesh.shape[a] for a in AXES)
    placed = (
        P("gx", "gy", "gz", None, None),
        P("gx", "gy", "gz", None),
        P("gx", "gy", "gz", None, None, None),
        P("gx", "gy", "gz", None, None),
        P("gx", "gy", "gz", None, None),
    )
    return jax.shard_map(
        functools.partial(on_device, sizes),
        mesh=mesh,
        in_specs=placed,
        out_specs=(P("gx", "gy", "gz", None, None), P()),
        check_vma=False,
    )
```

time: 49.3 us -> 44.6 us (0.905)
  Pallas kernels: 48.5 us -> 43.8 us
    pallas_call x1, Pallas kernels: 46.3 us -> 42.4 us  [on_device(): pl.pallas_call(functools.partial(kernel, sizes), out_shape=(jax.ShapeDtyp...]
    pallas_call x1, Pallas kernels: 2.18 us -> 1.46 us  [on_device(): pl.pallas_call(combine, out_shape=(jax.ShapeDtypeStruct((nblk, blk, cols)...]
where the time goes in v2:
time: 44.6 us; the launch traced here: 44.5 us
  Pallas kernels  43.8 us (98%)
  between operations  0.64 us (1%)
    pallas_call x1, Pallas kernels, on_device(): pl.pallas_call(functools.partial(kernel, sizes), out_shape=(jax.ShapeDtyp...  42.4 us
    pallas_call x1, Pallas kernels, on_device(): pl.pallas_call(combine, out_shape=(jax.ShapeDtypeStruct((nblk, blk, cols)...  1.46 us

profile of v2, /device:TPU:0, one launch (start us, length us, event | category | flops | bytes accessed | tf_op | source)
XLA Modules:
  0.0 44.5 jit_solution(8414910509552672682)
XLA Ops:
  0.6 42.4 %shard_map.68 = (f32[16,128,256]{2,1,0:T(8,128)S(1)}, f32[16,128,256]{2,1,0:T(8,128)S(1)}, f32[3,256]{1,0:T(4,128)S(1)}) custom-call(s32[2,6]{1,0:T(2,128)} %bitcast.13, bf16[16,128,2048]{2,1,0:T(8,128)(2,1)} %bitcast.9, f32[16,1,128]{2,1,0:T(1,128)} %bitcast.12, f32[16,128,128]{2,1,0:T(8,128)} %bitcast.10, bf16[16,128,256]{2,1,0:T(8,128)(2,1)} %bitcast.11), custom_call_target="tpu_custom_call" | custom-call | tf_op jit(solution)/shard_map/pallas_call | solution.py:653
  43.0 1.5 %shard_map.69 = (f32[16,128,256]{2,1,0:T(8,128)}, f32[1,256]{1,0:T(1,128)}) custom-call(f32[16,128,256]{2,1,0:T(8,128)S(1)} %get-tuple-element.7.z1, f32[16,128,256]{2,1,0:T(8,128)S(1)} %get-tuple-element.8.z2, f32[3,256]{1,0:T(4,128)S(1)} %get-tuple-element.9.final), custom_call_target="tpu_custom_call" | custom-call | tf_op jit(solution)/shard_map/pallas_call | solution.py:712

commit v3 on v2

--- a/solution.py
+++ b/solution.py
@@ -13,7 +13,6 @@
 LANES = 128
 F32 = jnp.float32
 BF16 = jnp.bfloat16
-ORDER = (2, 3, 0, 1, 4, 5)
 NEAR = (4, 5, 0, 1)
 FAR = (2, 3)
 ALL = (0, 1, 2, 3, 4, 5)
@@ -52,7 +51,6 @@
     pass_first,
     pass_full,
     pass_half,
-    pass_last,
     sums,
     plane_one,
     line_one,
@@ -86,10 +84,6 @@
     ]
     for copy in local:
         copy.start()
-    for b in range(nblk):
-        pltpu.make_async_copy(
-            schur_hbm.at[:, :, pl.ds(b * blk, blk)], schur_all.at[b], local_sems.at[4]
-        ).start()
 
     def plane_peer(step):
         other = lax.rem(here + step, planes)
@@ -139,7 +133,7 @@
             middle = pass_full.at[groups - 1 + g]
             return g, groups + g, u1_send.at[g], u1_recv.at[g], middle, rows, 0, half
         if g == groups - 1:
-            return g, g, u2_send.at[g], u2_recv.at[g], pass_last, half, half, half // 4
+            return g, g, u2_send.at[g], u2_recv.at[g], None, half, half, 0
         return g, g, u2_send.at[g], u2_recv.at[g], pass_half.at[g], half, half, half // 2
 
     def before(kind, g):
@@ -176,25 +170,41 @@
     def sent(msg, d):
         face(msg, d, d ^ 1, target[d]).wait_send()
 
+    def send_far(kind, g, begin=0, end=None):
+        msg = message(kind, g)
+        count, via = msg[5], msg[7]
+        end = end or count
+        for d in FAR:
+            @pl.when(has[d])
+            def _(d=d):
+                if before(kind, g):
+                    sent(message(*before(kind, g)), d)
+
+        if relayed:
+            for d in FAR:
+                @pl.when(gy == ends(d)[0])
+                def _(d=d):
+                    if via and end == count:
+                        to_relay(msg, d).start()
+                    if begin < count - via:
+                        size = min(end, count - via) - begin
+                        face(msg, d, d ^ 1, target[d], begin, size).start()
+
+        for d in FAR:
+            plain = jnp.logical_and(has[d], gy != ends(d)[0]) if relayed else has[d]
+
+            @pl.when(plain)
+            def _(d=d):
+                face(msg, d, d ^ 1, target[d], begin, end - begin).start()
+
     def send(kind, g, d):
         msg = message(kind, g)
-        count, via = msg[5], msg[7]
 
         @pl.when(has[d])
         def _():
             if before(kind, g):
                 sent(message(*before(kind, g)), d)
-            if relayed and d in FAR:
-                @pl.when(gy == ends(d)[0])
-                def _():
-                    to_relay(msg, d).start()
-                    face(msg, d, d ^ 1, target[d], 0, count - via).start()
-
-                @pl.when(gy != ends(d)[0])
-                def _():
-                    face(msg, d, d ^ 1, target[d]).start()
-            else:
-                face(msg, d, d ^ 1, target[d]).start()
+            face(msg, d, d ^ 1, target[d]).start()
 
     def forward(msg, d):
         g, number, _, landing, middle, count, _, via = msg
@@ -208,9 +218,9 @@
         )
 
     def relay(kind, g):
-        if not relayed:
+        msg = message(kind, g)
+        if not relayed or not msg[7]:
             return
-        msg = message(kind, g)
         for d in FAR:
             @pl.when(gy == ends(d)[1])
             def _(d=d):
@@ -222,6 +232,13 @@
     def arrived(kind, g, d):
         face(message(kind, g), d, d, target[d]).wait_recv()
 
+    def relay_sent(msg):
+        if relayed and msg[7]:
+            for d in FAR:
+                @pl.when(gy == ends(d)[1])
+                def _(d=d):
+                    forward(msg, d).wait_send()
+
     def all_sent(kind, g):
         msg = message(kind, g)
         for d in range(6):
@@ -229,11 +246,7 @@
             def _(d=d):
                 sent(msg, d)
 
-        if relayed:
-            for d in FAR:
-                @pl.when(gy == ends(d)[1])
-                def _(d=d):
-                    forward(msg, d).wait_send()
+        relay_sent(msg)
 
     def reduce_start(number, buf, count, me, peer, send_sem, recv_sem):
         for step in range(1, count):
@@ -313,14 +326,14 @@
     local[1].wait()
     for d in FAR:
         gather_load(0, d)
+    pl.semaphore_wait(barrier, entered)
+    send_far("load", 0, 0, rows)
     local[2].wait()
     for d in FAR:
         gather_prec(d)
     gather_load(0, 0)
     gather_prec(0)
-    pl.semaphore_wait(barrier, entered)
-    for d in FAR:
-        send("load", 0, d)
+    send_far("load", 0, rows, 2 * rows)
     gather_load(0, 1)
     gather_prec(1)
     send("load", 0, 0)
@@ -330,6 +343,10 @@
     gather_load(0, 5)
     gather_prec(5)
     send("load", 0, 4)
+    for b in range(nblk):
+        pltpu.make_async_copy(
+            schur_hbm.at[:, :, pl.ds(b * blk, blk)], schur_all.at[b], local_sems.at[4]
+        ).start()
     for g in range(1, groups):
         for d in range(6):
             gather_load(g, d)
@@ -354,7 +371,8 @@
         diag_slots[s * blk : (s + 1) * blk] = jnp.broadcast_to(column, (blk, lanes))
     relay("load", 0)
     for g in range(1, groups):
-        for d in ORDER:
+        send_far("load", g)
+        for d in (0, 1, 4, 5):
             send("load", g, d)
     pltpu.make_async_copy(schur_all, schur_all, local_sems.at[4]).wait()
     for s in range(slots):
@@ -439,8 +457,7 @@
             def _(d=d):
                 add_diagonal(z_ref, u_ref, g, d)
 
-        for d in FAR:
-            send(kind, g, d)
+        send_far(kind, g)
 
     def finish_near(g, z_ref, u_ref, kind):
         for d in FAR:
@@ -568,6 +585,7 @@
     reduce_start(1, plane_two, *plane_args)
     for g in range(groups):
         all_sent("two", g)
+    relay_sent(message("one", last))
     reduce_wait(0, plane_one, *plane_args, True)
     reduce_wait(0, line_one, *line_args, True)
     reduce_middle(1)
@@ -619,14 +637,13 @@
 def combine(z1, z2, final, out_ref, norm_ref, buf, norm_buf, sems):
     nblk = out_ref.shape[0]
     norm_buf[...] = final[2:3]
-    copies = [pltpu.make_async_copy(norm_buf, norm_ref, sems.at[nblk])]
-    copies[0].start()
+    norm_copy = pltpu.make_async_copy(norm_buf, norm_ref, sems.at[1])
+    norm_copy.start()
     for b in range(nblk):
         buf[b] = final[0:1] * z1[b] + final[1:2] * z2[b]
-        copies.append(pltpu.make_async_copy(buf.at[b], out_ref.at[b], sems.at[b]))
-        copies[-1].start()
-    for copy in copies:
-        copy.wait()
+        pltpu.make_async_copy(buf.at[b], out_ref.at[b], sems.at[0]).start()
+    pltpu.make_async_copy(buf, out_ref, sems.at[0]).wait()
+    norm_copy.wait()
 
 
 def in_hbm(x):
@@ -683,7 +700,6 @@
             vmem((rows, LANES), F32),
             vmem((2 * groups - 1, rows // 2, LANES), F32),
             vmem((max(groups - 1, 1), rows // 4, LANES), F32),
-            vmem((rows // 8, LANES), F32),
             vmem((groups, 6, 8, LANES), F32),
             vmem((planes, 2 * groups, LANES), F32),
             vmem((nx, 2 * groups, LANES), F32),
@@ -717,7 +733,7 @@
         ),
         in_specs=[local, local, local],
         out_specs=(hbm, hbm),
-        scratch_shapes=[vmem((nblk, blk, cols), F32), vmem((1, cols), F32), dma((nblk + 1,))],
+        scratch_shapes=[vmem((nblk, blk, cols), F32), vmem((1, cols), F32), dma((2,))],
         compiler_params=pltpu.CompilerParams(vmem_limit_bytes=16 * mib),
     )(z1, z2, final)
     return result.reshape(1, 1, 1, nblk * blk, cols), norm.reshape(cols)

time: 44.6 us -> 42.9 us (0.962)
  Pallas kernels: 43.8 us -> 42.1 us
    pallas_call x1, Pallas kernels: 42.4 us -> 40.8 us  [on_device(): pl.pallas_call(functools.partial(kernel, sizes), out_shape=(jax.ShapeDtyp...]
where the time goes in v3:
time: 42.9 us; the launch traced here: 42.7 us
  Pallas kernels  42.1 us (98%)
  between operations  0.64 us (1%)
    pallas_call x1, Pallas kernels, on_device(): pl.pallas_call(functools.partial(kernel, sizes), out_shape=(jax.ShapeDtyp...  40.8 us
    pallas_call x1, Pallas kernels, on_device(): pl.pallas_call(combine, out_shape=(jax.ShapeDtypeStruct((nblk, blk, cols)...  1.33 us

profile of v3, /device:TPU:0, one launch (start us, length us, event | category | flops | bytes accessed | tf_op | source)
XLA Modules:
  0.0 42.7 jit_solution(16856376322084038259)
XLA Ops:
  0.6 40.8 %shard_map.68 = (f32[16,128,256]{2,1,0:T(8,128)S(1)}, f32[16,128,256]{2,1,0:T(8,128)S(1)}, f32[3,256]{1,0:T(4,128)S(1)}) custom-call(s32[2,6]{1,0:T(2,128)} %bitcast.13, bf16[16,128,2048]{2,1,0:T(8,128)(2,1)} %bitcast.9, f32[16,1,128]{2,1,0:T(1,128)} %bitcast.12, f32[16,128,128]{2,1,0:T(8,128)} %bitcast.10, bf16[16,128,256]{2,1,0:T(8,128)(2,1)} %bitcast.11), custom_call_target="tpu_custom_call" | custom-call | tf_op jit(solution)/shard_map/pallas_call | solution.py:670
  41.4 1.3 %shard_map.69 = (f32[16,128,256]{2,1,0:T(8,128)}, f32[1,256]{1,0:T(1,128)}) custom-call(f32[16,128,256]{2,1,0:T(8,128)S(1)} %get-tuple-element.7.z1, f32[16,128,256]{2,1,0:T(8,128)S(1)} %get-tuple-element.8.z2, f32[3,256]{1,0:T(4,128)S(1)} %get-tuple-element.9.final), custom_call_target="tpu_custom_call" | custom-call | tf_op jit(solution)/shard_map/pallas_call | solution.py:728

commit v4 on v3

--- a/solution.py
+++ b/solution.py
@@ -248,55 +248,96 @@
 
         relay_sent(msg)
 
-    def reduce_start(number, buf, count, me, peer, send_sem, recv_sem):
-        for step in range(1, count):
-            pltpu.make_async_remote_copy(
-                src_ref=buf.at[me],
-                dst_ref=buf.at[me],
-                send_sem=send_sem.at[number],
-                recv_sem=recv_sem.at[number],
-                device_id=peer(step),
-                device_id_type=MESH,
-            ).start()
-
-    def reduce_wait(number, buf, count, me, peer, send_sem, recv_sem, sent):
-        if count > 1:
-            copy = pltpu.make_async_remote_copy(
-                src_ref=buf.at[pl.ds(0, count - 1)],
-                dst_ref=buf.at[pl.ds(0, count - 1)],
-                send_sem=send_sem.at[number],
-                recv_sem=recv_sem.at[number],
-                device_id=peer(1),
-                device_id_type=MESH,
+    def plane_of(number):
+        return plane_two if number else plane_one
+
+    def line_of(number):
+        return line_two if number else line_one
+
+    def part_copy(number, buf, slot, device, send_sem, recv_sem):
+        return pltpu.make_async_remote_copy(
+            src_ref=buf.at[slot],
+            dst_ref=buf.at[slot],
+            send_sem=send_sem.at[number],
+            recv_sem=recv_sem.at[number],
+            device_id=device,
+            device_id_type=MESH,
+        )
+
+    def parts_wait(number, count, send_sem, recv_sem, sent):
+        if count:
+            buf = plane_of(number)
+            copy = part_copy(
+                number, buf, pl.ds(0, count), line_peer(1), send_sem, recv_sem
             )
             if sent:
                 copy.wait_send()
             else:
                 copy.wait_recv()
 
-    plane_args = (planes, here, plane_peer, plane_send, plane_recv)
-    line_args = (nx, gx, line_peer, line_send, line_recv)
-
-    def plane_of(number):
-        return plane_two if number else plane_one
-
-    def line_of(number):
-        return line_two if number else line_one
+    hub = nz - 1
+    is_hub = gz == hub
+
+    def reduce_start(number):
+        buf = plane_of(number)
+        if not relayed:
+            for step in range(1, planes):
+                part_copy(number, buf, here, plane_peer(step), plane_send, plane_recv).start()
+            return
+        for step in range(1, ny):
+            device = (gx, lax.rem(gy + step, ny), hub)
+            part_copy(number, buf, here, device, plane_send, plane_recv).start()
+
+        @pl.when(jnp.logical_not(is_hub))
+        def _():
+            part_copy(number, buf, here, (gx, gy, hub), plane_send, plane_recv).start()
+
+    def reduce_middle(number):
+        line = line_of(number)
+        if not relayed:
+            parts_wait(number, planes - 1, plane_send, plane_recv, False)
+            line[gx] = total_of(plane_of(number), planes)
+            for step in range(1, nx):
+                part_copy(number, line, gx, line_peer(step), line_send, line_recv).start()
+            return
+
+        @pl.when(is_hub)
+        def _():
+            parts_wait(number, planes - 1, plane_send, plane_recv, False)
+            line[gx] = total_of(plane_of(number), planes)
+            for core in range(nz):
+                for step in range(1, nx):
+                    device = (lax.rem(gx + nx - step, nx), gy, core)
+                    part_copy(number, line, gx, device, line_send, line_recv).start()
+            part_copy(number, line, gx, (gx, gy, 0), line_send, line_recv).start()
+
+    def reduce_end(number):
+        if relayed:
+            for core in range(nz):
+                @pl.when(gz == core)
+                def _(core=core):
+                    parts_wait(number, nx - (core == hub), line_send, line_recv, False)
+        else:
+            parts_wait(number, nx - 1, line_send, line_recv, False)
+        return total_of(line_of(number), nx)
+
+    def reduce_sent(number):
+        if not relayed:
+            parts_wait(number, planes - 1, plane_send, plane_recv, True)
+            parts_wait(number, nx - 1, line_send, line_recv, True)
+            return
+        for core in range(nz):
+            @pl.when(gz == core)
+            def _(core=core):
+                parts_wait(number, ny - (core == hub), plane_send, plane_recv, True)
+                if core == hub:
+                    parts_wait(number, nz * (nx - 1) + 1, line_send, line_recv, True)
 
     def total_of(buf, count):
         total = buf[0]
         for i in range(1, count):
             total = total + buf[i]
         return total
-
-    def reduce_middle(number):
-        reduce_wait(number, plane_of(number), *plane_args, False)
-        line_of(number)[gx] = total_of(plane_of(number), planes)
-        reduce_start(number, line_of(number), *line_args)
-
-    def reduce_end(number):
-        reduce_wait(number, line_of(number), *line_args, False)
-        return total_of(line_of(number), nx)
 
     def folded(x):
         return jnp.sum(x.reshape(x.shape[0] // 8, 8, lanes), axis=0)
@@ -518,7 +559,7 @@
         if g == 0:
             packed = [pack((0.5 * sums[i, 0], sums[i, 1])) for i in range(groups)]
             plane_one[here] = jnp.concatenate(packed, axis=0)
-            reduce_start(0, plane_one, *plane_args)
+            reduce_start(0)
             if groups > 1:
                 relay("one", last)
         else:
@@ -582,14 +623,12 @@
     for g in range(groups):
         packed.append(pack((0.5 * sums[g, 2], sums[g, 3], sums[g, 4], sums[g, 5])))
     plane_two[here] = jnp.concatenate(packed, axis=0)
-    reduce_start(1, plane_two, *plane_args)
+    reduce_start(1)
     for g in range(groups):
         all_sent("two", g)
     relay_sent(message("one", last))
-    reduce_wait(0, plane_one, *plane_args, True)
-    reduce_wait(0, line_one, *line_args, True)
+    reduce_sent(0)
     reduce_middle(1)
-    reduce_wait(1, plane_two, *plane_args, True)
     total = reduce_end(1)
 
     def both(rows_of):
@@ -631,7 +670,7 @@
     final_ref[0:1] = y1 * inverse - weight2 * h11
     final_ref[1:2] = weight2
     final_ref[2:3] = beta * s1 * s2
-    reduce_wait(1, line_two, *line_args, True)
+    reduce_sent(1)
 
 
 def combine(z1, z2, final, out_ref, norm_ref, buf, norm_buf, sems):

time: 42.9 us -> 42 us (0.979)
  Pallas kernels: 42.1 us -> 41.2 us
    pallas_call x1, Pallas kernels: 40.8 us -> 39.9 us  [on_device(): pl.pallas_call(functools.partial(kernel, sizes), out_shape=(jax.ShapeDtyp...]
where the time goes in v4:
time: 42 us; the launch traced here: 41.9 us
  Pallas kernels  41.2 us (98%)
  between operations  0.64 us (2%)
    pallas_call x1, Pallas kernels, on_device(): pl.pallas_call(functools.partial(kernel, sizes), out_shape=(jax.ShapeDtyp...  39.9 us
    pallas_call x1, Pallas kernels, on_device(): pl.pallas_call(combine, out_shape=(jax.ShapeDtypeStruct((nblk, blk, cols)...  1.33 us

profile of v4, /device:TPU:0, one launch (start us, length us, event | category | flops | bytes accessed | tf_op | source)
XLA Modules:
  0.0 41.9 jit_solution(15137675469870017287)
XLA Ops:
  0.6 39.9 %shard_map.68 = (f32[16,128,256]{2,1,0:T(8,128)S(1)}, f32[16,128,256]{2,1,0:T(8,128)S(1)}, f32[3,256]{1,0:T(4,128)S(1)}) custom-call(s32[2,6]{1,0:T(2,128)} %bitcast.13, bf16[16,128,2048]{2,1,0:T(8,128)(2,1)} %bitcast.9, f32[16,1,128]{2,1,0:T(1,128)} %bitcast.12, f32[16,128,128]{2,1,0:T(8,128)} %bitcast.10, bf16[16,128,256]{2,1,0:T(8,128)(2,1)} %bitcast.11), custom_call_target="tpu_custom_call" | custom-call | tf_op jit(solution)/shard_map/pallas_call | solution.py:709
  40.5 1.3 %shard_map.69 = (f32[16,128,256]{2,1,0:T(8,128)}, f32[1,256]{1,0:T(1,128)}) custom-call(f32[16,128,256]{2,1,0:T(8,128)S(1)} %get-tuple-element.7.z1, f32[16,128,256]{2,1,0:T(8,128)S(1)} %get-tuple-element.8.z2, f32[3,256]{1,0:T(4,128)S(1)} %get-tuple-element.9.final), custom_call_target="tpu_custom_call" | custom-call | tf_op jit(solution)/shard_map/pallas_call | solution.py:767

commit v5 on v4

--- a/solution.py
+++ b/solution.py
@@ -50,7 +50,6 @@
     u2_recv,
     pass_first,
     pass_full,
-    pass_half,
     sums,
     plane_one,
     line_one,
@@ -126,28 +125,25 @@
 
     def message(kind, g):
         if kind == "load" and g == 0:
-            return g, g, first_send, first_recv, pass_first, 2 * rows, 0, rows
+            return g, g, first_send, first_recv, pass_first, 2 * rows, rows
         if kind == "load":
-            return g, g, load_send.at[g - 1], load_recv.at[g - 1], pass_full.at[g - 1], rows, 0, half
+            return g, g, load_send.at[g - 1], load_recv.at[g - 1], pass_full.at[g - 1], rows, half
         if kind == "one":
             middle = pass_full.at[groups - 1 + g]
-            return g, groups + g, u1_send.at[g], u1_recv.at[g], middle, rows, 0, half
-        if g == groups - 1:
-            return g, g, u2_send.at[g], u2_recv.at[g], None, half, half, 0
-        return g, g, u2_send.at[g], u2_recv.at[g], pass_half.at[g], half, half, half // 2
+            return g, groups + g, u1_send.at[g], u1_recv.at[g], middle, rows, half
+        return g, g, u2_send.at[g], u2_recv.at[g], None, rows, 0
 
     def before(kind, g):
-        return {"load": None, "one": ("load", g), "two": ("one", g)}[kind]
+        return ("load", g) if kind == "one" else None
 
     def ends(d):
         return (1, 3, 2) if d == 2 else (2, 0, 1)
 
     def face(msg, d, slot, device, row=0, size=None):
-        g, number, source, landing, _, count, shift, _ = msg
+        g, number, source, landing, _, count, _ = msg
         size = size or count
-        begin = (shift if d % 2 == 0 else 0) + row
         return pltpu.make_async_remote_copy(
-            src_ref=source.at[d, pl.ds(begin, size)],
+            src_ref=source.at[d, pl.ds(row, size)],
             dst_ref=landing.at[slot, pl.ds(row, size)],
             send_sem=face_send.at[g, d],
             recv_sem=face_recv.at[number, slot],
@@ -156,10 +152,9 @@
         )
 
     def to_relay(msg, d):
-        g, number, source, _, middle, count, shift, via = msg
-        begin = (shift if d % 2 == 0 else 0) + count - via
+        g, number, source, _, middle, count, via = msg
         return pltpu.make_async_remote_copy(
-            src_ref=source.at[d, pl.ds(begin, via)],
+            src_ref=source.at[d, pl.ds(count - via, via)],
             dst_ref=middle,
             send_sem=face_send.at[g, d],
             recv_sem=pass_recv.at[number],
@@ -167,12 +162,50 @@
             device_id_type=MESH,
         )
 
+    def cuts(d):
+        if relayed and d in FAR:
+            low, high = rows // 4, rows - rows // 4
+            if d == 2:
+                return ((gy == 0, low), (gy == 1, half), (gy == 2, high))
+            return ((gy == 1, low), (gy == 2, half), (gy == 3, high))
+        return ((has[d], half),)
+
+    def share(d, cut):
+        return (cut, rows - cut) if d % 2 == 0 else (0, cut)
+
+    def own(d, cut):
+        return (0, cut) if d % 2 == 0 else (cut, rows - cut)
+
+    def two_copy(g, d, cut):
+        return face(message("two", g), d, d ^ 1, target[d], *share(d, cut))
+
+    def two_send(g, faces):
+        msg = message("two", g)
+        todo = [(d, here_is, cut) for d in faces for here_is, cut in cuts(d)]
+        todo.sort(key=lambda item: not (relayed and item[0] in FAR and item[2] == half))
+        for d in faces:
+            @pl.when(has[d])
+            def _(d=d):
+                sent(message("one", g), d)
+
+        for d, here_is, cut in todo:
+            @pl.when(here_is)
+            def _(d=d, cut=cut):
+                two_copy(g, d, cut).start()
+
+    def two_sent(g):
+        for d in range(6):
+            for here_is, cut in cuts(d):
+                @pl.when(here_is)
+                def _(d=d, cut=cut):
+                    two_copy(g, d, cut).wait_send()
+
     def sent(msg, d):
         face(msg, d, d ^ 1, target[d]).wait_send()
 
     def send_far(kind, g, begin=0, end=None):
         msg = message(kind, g)
-        count, via = msg[5], msg[7]
+        count, via = msg[5], msg[6]
         end = end or count
         for d in FAR:
             @pl.when(has[d])
@@ -207,7 +240,7 @@
             face(msg, d, d ^ 1, target[d]).start()
 
     def forward(msg, d):
-        g, number, _, landing, middle, count, _, via = msg
+        g, number, _, landing, middle, count, via = msg
         return pltpu.make_async_remote_copy(
             src_ref=middle,
             dst_ref=landing.at[d ^ 1, pl.ds(count - via, via)],
@@ -219,7 +252,7 @@
 
     def relay(kind, g):
         msg = message(kind, g)
-        if not relayed or not msg[7]:
+        if not relayed or not msg[6]:
             return
         for d in FAR:
             @pl.when(gy == ends(d)[1])
@@ -233,20 +266,11 @@
         face(message(kind, g), d, d, target[d]).wait_recv()
 
     def relay_sent(msg):
-        if relayed and msg[7]:
+        if relayed and msg[6]:
             for d in FAR:
                 @pl.when(gy == ends(d)[1])
                 def _(d=d):
                     forward(msg, d).wait_send()
-
-    def all_sent(kind, g):
-        msg = message(kind, g)
-        for d in range(6):
-            @pl.when(has[d])
-            def _(d=d):
-                sent(msg, d)
-
-        relay_sent(msg)
 
     def plane_of(number):
         return plane_two if number else plane_one
@@ -288,9 +312,12 @@
             device = (gx, lax.rem(gy + step, ny), hub)
             part_copy(number, buf, here, device, plane_send, plane_recv).start()
 
-        @pl.when(jnp.logical_not(is_hub))
-        def _():
-            part_copy(number, buf, here, (gx, gy, hub), plane_send, plane_recv).start()
+    def reduce_own(number):
+        if relayed:
+            @pl.when(jnp.logical_not(is_hub))
+            def _():
+                buf = plane_of(number)
+                part_copy(number, buf, here, (gx, gy, hub), plane_send, plane_recv).start()
 
     def reduce_middle(number):
         line = line_of(number)
@@ -492,15 +519,13 @@
         scale = diag_slots[d * rows : (d + 1) * rows]
         u_ref[g, d] = u_ref[g, d] + scale * z_ref[g, d * cap : (d + 1) * cap].reshape(rows, lanes)
 
-    def finish_far(g, z_ref, u_ref, kind):
+    def finish_far(g, z_ref, u_ref):
         for d in FAR:
             @pl.when(has[d])
             def _(d=d):
                 add_diagonal(z_ref, u_ref, g, d)
 
-        send_far(kind, g)
-
-    def finish_near(g, z_ref, u_ref, kind):
+    def finish_near(g, z_ref, u_ref):
         for d in FAR:
             @pl.when(has[d])
             def _(d=d):
@@ -513,8 +538,9 @@
             def _(d=d):
                 add_diagonal(z_ref, u_ref, g, d)
 
+    def send_near(g):
         for d in (0, 1, 4, 5):
-            send(kind, g, d)
+            send("one", g, d)
 
     def cross(g):
         for d in range(6):
@@ -546,9 +572,20 @@
             relay("one", g - 1)
         for d in FAR:
             first_step(g, d)
-        finish_far(g, z1_ref, u1_send, "one")
-        finish_near(g, z1_ref, u1_send, "one")
-        cross(g)
+        finish_far(g, z1_ref, u1_send)
+        if g < last:
+            send_far("one", g)
+            finish_near(g, z1_ref, u1_send)
+            send_near(g)
+            cross(g)
+        else:
+            finish_near(g, z1_ref, u1_send)
+            cross(g)
+            packed = [pack((0.5 * sums[i, 0], sums[i, 1])) for i in range(groups)]
+            plane_one[here] = jnp.concatenate(packed, axis=0)
+            reduce_start(0)
+            send_far("one", g)
+            send_near(g)
         spread(g, z1_ref, z1_out)
 
     for g in range(groups):
@@ -556,20 +593,21 @@
             relay("one", last)
         for d in NEAR:
             second_step(g, d)
+        if g:
+            two_send(g - 1, FAR)
         if g == 0:
-            packed = [pack((0.5 * sums[i, 0], sums[i, 1])) for i in range(groups)]
-            plane_one[here] = jnp.concatenate(packed, axis=0)
-            reduce_start(0)
+            reduce_own(0)
             if groups > 1:
                 relay("one", last)
-        else:
-            relay("two", g - 1)
         for d in FAR:
             second_step(g, d)
-        finish_far(g, z2_ref, u2_send, "two")
+        finish_far(g, z2_ref, u2_send)
         if g == last:
+            two_send(g, FAR)
+        finish_near(g, z2_ref, u2_send)
+        two_send(g, (0, 1, 4, 5))
+        if g == 0:
             reduce_middle(0)
-        finish_near(g, z2_ref, u2_send, "two")
 
     def measure(g, h11):
         for d in range(6):
@@ -591,21 +629,22 @@
                 add_sum(g, 4, second)
 
     def third_step(g, d, h11):
-        @pl.when(has[d])
-        def _():
-            arrived("two", g, d)
-            begin = 0 if d % 2 == 0 else half
-            work = jnp.zeros((8, lanes), F32)
-            size = min(half, blk)
-            for row in range(0, half, size):
-                at = slice(begin + row, begin + row + size)
-                w = (u2_send[g, d, at] + u2_recv[g, d, row : row + size]) * mask[d * cap + (begin + row) // blk]
-                w = w - h11 * a_ref[g, d, at]
-                work = work + folded(w * w)
-            add_sum(g, 5, work)
+        for here_is, cut in cuts(d):
+            @pl.when(here_is)
+            def _(cut=cut):
+                begin, size = own(d, cut)
+                face(message("two", g), d, d, target[d], begin, size).wait_recv()
+                work = jnp.zeros((8, lanes), F32)
+                for k in range(cap):
+                    first, last = max(begin, k * blk), min(begin + size, (k + 1) * blk)
+                    if first < last:
+                        at = slice(first, last)
+                        w = (u2_send[g, d, at] + u2_recv[g, d, at]) * mask[d * cap + k]
+                        w = w - h11 * a_ref[g, d, at]
+                        work = work + folded(w * w)
+                add_sum(g, 5, work)
 
     spread(0, z2_ref, z2_out)
-    relay("two", last)
     total = reduce_end(0)
     squares = [total[2 * g : 2 * g + 1] for g in range(groups)]
     inners = [total[2 * g + 1 : 2 * g + 2] / (squares[g] + EPS) for g in range(groups)]
@@ -624,9 +663,10 @@
         packed.append(pack((0.5 * sums[g, 2], sums[g, 3], sums[g, 4], sums[g, 5])))
     plane_two[here] = jnp.concatenate(packed, axis=0)
     reduce_start(1)
+    reduce_own(1)
     for g in range(groups):
-        all_sent("two", g)
-    relay_sent(message("one", last))
+        two_sent(g)
+        relay_sent(message("one", g))
     reduce_sent(0)
     reduce_middle(1)
     total = reduce_end(1)
@@ -735,10 +775,9 @@
             vmem((groups, 6, rows, LANES), F32),
             vmem((groups, 6, rows, LANES), F32),
             vmem((groups, 6, rows, LANES), F32),
-            vmem((groups, 6, rows // 2, LANES), F32),
+            vmem((groups, 6, rows, LANES), F32),
             vmem((rows, LANES), F32),
             vmem((2 * groups - 1, rows // 2, LANES), F32),
-            vmem((max(groups - 1, 1), rows // 4, LANES), F32),
             vmem((groups, 6, 8, LANES), F32),
             vmem((planes, 2 * groups, LANES), F32),
             vmem((nx, 2 * groups, LANES), F32),

time: 42 us -> 41.4 us (0.986)
  Pallas kernels: 41.2 us -> 40.6 us
    pallas_call x1, Pallas kernels: 39.9 us -> 39.3 us  [on_device(): pl.pallas_call(functools.partial(kernel, sizes), out_shape=(jax.ShapeDtyp...]
where the time goes in v5:
time: 41.4 us; the launch traced here: 41.2 us
  Pallas kernels  40.6 us (98%)
  between operations  0.64 us (2%)
    pallas_call x1, Pallas kernels, on_device(): pl.pallas_call(functools.partial(kernel, sizes), out_shape=(jax.ShapeDtyp...  39.3 us
    pallas_call x1, Pallas kernels, on_device(): pl.pallas_call(combine, out_shape=(jax.ShapeDtypeStruct((nblk, blk, cols)...  1.33 us

profile of v5, /device:TPU:0, one launch (start us, length us, event | category | flops | bytes accessed | tf_op | source)
XLA Modules:
  0.0 41.2 jit_solution(2203891407653684203)
XLA Ops:
  0.6 39.3 %shard_map.68 = (f32[16,128,256]{2,1,0:T(8,128)S(1)}, f32[16,128,256]{2,1,0:T(8,128)S(1)}, f32[3,256]{1,0:T(4,128)S(1)}) custom-call(s32[2,6]{1,0:T(2,128)} %bitcast.13, bf16[16,128,2048]{2,1,0:T(8,128)(2,1)} %bitcast.9, f32[16,1,128]{2,1,0:T(1,128)} %bitcast.12, f32[16,128,128]{2,1,0:T(8,128)} %bitcast.10, bf16[16,128,256]{2,1,0:T(8,128)(2,1)} %bitcast.11), custom_call_target="tpu_custom_call" | custom-call | tf_op jit(solution)/shard_map/pallas_call | solution.py:749
  39.9 1.3 %shard_map.69 = (f32[16,128,256]{2,1,0:T(8,128)}, f32[1,256]{1,0:T(1,128)}) custom-call(f32[16,128,256]{2,1,0:T(8,128)S(1)} %get-tuple-element.7.z1, f32[16,128,256]{2,1,0:T(8,128)S(1)} %get-tuple-element.8.z2, f32[3,256]{1,0:T(4,128)S(1)} %get-tuple-element.9.final), custom_call_target="tpu_custom_call" | custom-call | tf_op jit(solution)/shard_map/pallas_call | solution.py:806

commit v6 on v5

--- a/solution.py
+++ b/solution.py
@@ -81,8 +81,13 @@
         pltpu.make_async_copy(source, target, local_sems.at[i])
         for i, (source, target) in enumerate(moves)
     ]
-    for copy in local:
-        copy.start()
+    local[0].start()
+    pieces = 4 if nblk % 4 == 0 else 1
+    for source, goal, sem in ((load_hbm, load_all, 1), (prec_hbm, prec_all, 2)):
+        for i in range(pieces):
+            at = pl.ds(i * (nblk // pieces), nblk // pieces)
+            pltpu.make_async_copy(source.at[at], goal.at[at], local_sems.at[sem]).start()
+    local[3].start()
 
     def plane_peer(step):
         other = lax.rem(here + step, planes)
@@ -136,6 +141,9 @@
     def before(kind, g):
         return ("load", g) if kind == "one" else None
 
+    def sem_of(d):
+        return 4 if nz == 2 and d == 5 else d
+
     def ends(d):
         return (1, 3, 2) if d == 2 else (2, 0, 1)
 
@@ -145,8 +153,8 @@
         return pltpu.make_async_remote_copy(
             src_ref=source.at[d, pl.ds(row, size)],
             dst_ref=landing.at[slot, pl.ds(row, size)],
-            send_sem=face_send.at[g, d],
-            recv_sem=face_recv.at[number, slot],
+            send_sem=face_send.at[g, sem_of(d)],
+            recv_sem=face_recv.at[number, sem_of(slot)],
             device_id=device,
             device_id_type=MESH,
         )
@@ -156,7 +164,7 @@
         return pltpu.make_async_remote_copy(
             src_ref=source.at[d, pl.ds(count - via, via)],
             dst_ref=middle,
-            send_sem=face_send.at[g, d],
+            send_sem=face_send.at[g, sem_of(d)],
             recv_sem=pass_recv.at[number],
             device_id=(gx, ends(d)[1], gz),
             device_id_type=MESH,
@@ -245,7 +253,7 @@
             src_ref=middle,
             dst_ref=landing.at[d ^ 1, pl.ds(count - via, via)],
             send_sem=pass_send.at[g],
-            recv_sem=face_recv.at[number, d ^ 1],
+            recv_sem=face_recv.at[number, sem_of(d ^ 1)],
             device_id=(gx, ends(d)[2], gz),
             device_id_type=MESH,
         )
@@ -475,8 +483,20 @@
     def columns_of(z_ref, g, d):
         return narrowed([z_ref[g, d * cap + k] for k in range(cap)])
 
-    def first_step(g, d):
-        @pl.when(has[d])
+    def far_steps(step, g):
+        if not relayed:
+            for d in FAR:
+                step(g, d, has[d], FAR)
+            return
+        step(g, 3, gy == 1, ALL)
+        step(g, 2, gy == 2, ALL)
+        step(g, 2, gy <= 1, FAR)
+        step(g, 3, gy >= 2, FAR)
+
+    late = ((2, gy <= 1), (3, gy >= 2)) if relayed else tuple((d, has[d]) for d in FAR)
+
+    def first_step(g, d, here_is, which):
+        @pl.when(here_is)
         def _():
             arrived("load", g, d)
             if g == 0:
@@ -499,10 +519,10 @@
                 z.append(precondition(d * cap + k, value))
                 z1_ref[g, d * cap + k] = z[-1]
             add_sum(g, 0, square)
-            multiply(d, narrowed(z), u1_send.at[g], ALL if d in NEAR else FAR)
-
-    def second_step(g, d):
-        @pl.when(has[d])
+            multiply(d, narrowed(z), u1_send.at[g], which)
+
+    def second_step(g, d, here_is, which):
+        @pl.when(here_is)
         def _():
             arrived("one", g, d)
             z = []
@@ -513,7 +533,7 @@
                 a_ref[g, d, at] = value
                 z.append(precondition(s, value))
                 z2_ref[g, s] = z[-1]
-            multiply(d, narrowed(z), u2_send.at[g], ALL if d in NEAR else FAR)
+            multiply(d, narrowed(z), u2_send.at[g], which)
 
     def add_diagonal(z_ref, u_ref, g, d):
         scale = diag_slots[d * rows : (d + 1) * rows]
@@ -526,8 +546,8 @@
                 add_diagonal(z_ref, u_ref, g, d)
 
     def finish_near(g, z_ref, u_ref):
-        for d in FAR:
-            @pl.when(has[d])
+        for d, here_is in late:
+            @pl.when(here_is)
             def _(d=d):
                 narrow = columns_of(z_ref, g, d)
                 multiply(d, narrow, u_ref.at[g], (0, 1))
@@ -567,11 +587,10 @@
     last = groups - 1
     for g in range(groups):
         for d in NEAR:
-            first_step(g, d)
+            first_step(g, d, has[d], ALL)
         if g:
             relay("one", g - 1)
-        for d in FAR:
-            first_step(g, d)
+        far_steps(first_step, g)
         finish_far(g, z1_ref, u1_send)
         if g < last:
             send_far("one", g)
@@ -592,15 +611,14 @@
         if groups == 1:
             relay("one", last)
         for d in NEAR:
-            second_step(g, d)
+            second_step(g, d, has[d], ALL)
         if g:
             two_send(g - 1, FAR)
         if g == 0:
             reduce_own(0)
             if groups > 1:
                 relay("one", last)
-        for d in FAR:
-            second_step(g, d)
+        far_steps(second_step, g)
         finish_far(g, z2_ref, u2_send)
         if g == last:
             two_send(g, FAR)
@@ -784,8 +802,8 @@
             vmem((planes, 4 * groups, LANES), F32),
             vmem((nx, 4 * groups, LANES), F32),
             dma((5,)),
-            dma((groups, 6)),
-            dma((2 * groups, 6)),
+            dma((groups, 5 if nz == 2 else 6)),
+            dma((2 * groups, 5 if nz == 2 else 6)),
             dma((groups,)),
             dma((2 * groups,)),
             dma((2,)),

time: 41.4 us -> 41.4 us (level)
  no operation moved by 1% of the time
where the time goes in v6:
time: 41.4 us; the launch traced here: 41.2 us
  Pallas kernels  40.4 us (98%)
  between operations  0.8 us (2%)
    pallas_call x1, Pallas kernels, on_device(): pl.pallas_call(functools.partial(kernel, sizes), out_shape=(jax.ShapeDtyp...  39.1 us
    pallas_call x1, Pallas kernels, on_device(): pl.pallas_call(combine, out_shape=(jax.ShapeDtypeStruct((nblk, blk, cols)...  1.33 us

profile of v6, /device:TPU:0, one launch (start us, length us, event | category | flops | bytes accessed | tf_op | source)
XLA Modules:
  0.0 41.2 jit_solution(13237890636017964288)
XLA Ops:
  0.6 39.1 %shard_map.68 = (f32[16,128,256]{2,1,0:T(8,128)S(1)}, f32[16,128,256]{2,1,0:T(8,128)S(1)}, f32[3,256]{1,0:T(4,128)S(1)}) custom-call(s32[2,6]{1,0:T(2,128)} %bitcast.13, bf16[16,128,2048]{2,1,0:T(8,128)(2,1)} %bitcast.9, f32[16,1,128]{2,1,0:T(1,128)} %bitcast.12, f32[16,128,128]{2,1,0:T(8,128)} %bitcast.10, bf16[16,128,256]{2,1,0:T(8,128)(2,1)} %bitcast.11), custom_call_target="tpu_custom_call" | custom-call | tf_op jit(solution)/shard_map/pallas_call | solution.py:767
  39.7 1.3 %shard_map.69 = (f32[16,128,256]{2,1,0:T(8,128)}, f32[1,256]{1,0:T(1,128)}) custom-call(f32[16,128,256]{2,1,0:T(8,128)S(1)} %get-tuple-element.7.z1, f32[16,128,256]{2,1,0:T(8,128)S(1)} %get-tuple-element.8.z2, f32[3,256]{1,0:T(4,128)S(1)} %get-tuple-element.9.final), custom_call_target="tpu_custom_call" | custom-call | tf_op jit(solution)/shard_map/pallas_call | solution.py:824
